TPU v7x, 8 devices: a whole 2x2x1 slice. The times are simulated.
8 devices in a mesh: rep: 1 (over z), col: 2 (over y), row: 4 (over x, core).
Axes of the slice: x: 2, y: 2, z: 1, core: 2. Of those that a mesh axis runs over, the one named last changes fastest.
Arguments:
- hidden_0: bfloat16 [16, 6144], P('rep', 'row')
- hidden_1: bfloat16 [16, 6144], P('rep', 'row')
- positions: int32 [16], P(('rep', 'row'))
- lengths: int32 [16], P(('rep', 'row'))
- cache_k: bfloat16 [2, 16, 128, 8, 128], P(None, ('rep', 'row'), None, 'col')
- cache_v: bfloat16 [2, 16, 128, 8, 128], P(None, ('rep', 'row'), None, 'col')
- norm_attn: bfloat16 [2, 6144], P(None, 'row')
- norm_mlp: bfloat16 [2, 6144], P(None, 'row')
- w_query: bfloat16 [2, 6144, 6144], P(None, 'row', 'col')
- w_key: bfloat16 [2, 6144, 1024], P(None, 'row', 'col')
- w_value: bfloat16 [2, 6144, 1024], P(None, 'row', 'col')
- w_out: bfloat16 [2, 6144, 6144], P(None, 'row', 'col')
- w_gate: bfloat16 [2, 6144, 16384], P(None, 'row', 'col')
- w_up: bfloat16 [2, 6144, 16384], P(None, 'row', 'col')
- w_down: bfloat16 [2, 16384, 6144], P(None, 'row', 'col')
Outputs:
- output 1: bfloat16 [16, 6144], P('rep', 'row')
- output 2: bfloat16 [16, 6144], P('rep', 'row')
- output 3: bfloat16 [2, 16, 128, 8, 128], P(None, ('rep', 'row'), None, 'col')
- output 4: bfloat16 [2, 16, 128, 8, 128], P(None, ('rep', 'row'), None, 'col')
All inputs are finite; a program needn't handle non-finite values.
Results may differ from a plain program's by a relative error of at most 0.02.
Values are sent between devices in bfloat16 or wider.
A program may use at most 1 GiB of HBM per device.

v0:
```python
import jax
import jax.numpy as jnp
from jax import lax
from jax.sharding import PartitionSpec as P

ROPE_BASE = 1000000.0
EPS = 1e-05


def rope_rotate(vectors, positions):
    head_dim = vectors.shape[-1]
    half = head_dim // 2
    inv_freq = jnp.power(jnp.float32(ROPE_BASE), -jnp.arange(half, dtype=jnp.float32) * 2.0 / head_dim)
    angles = positions.astype(jnp.float32)[:, None, None] * inv_freq
    cosine = jnp.cos(angles)
    sine = jnp.sin(angles)
    vec_f32 = vectors.astype(jnp.float32)
    first = vec_f32[..., :half]
    second = vec_f32[..., half:]
    return jnp.concatenate([first * cosine - second * sine, second * cosine + first * sine], axis=-1).astype(jnp.bfloat16)


def add_residual(hidden, update):
    return (hidden.astype(jnp.float32) + update.astype(jnp.float32)).astype(jnp.bfloat16)


def attend_local(query, keys, vals, slots):
    scores = jnp.einsum('bkgd,blkd->bkgl', query, keys, preferred_element_type=jnp.float32) * (keys.shape[-1] ** -0.5)
    valid = jnp.arange(keys.shape[1])[None, None, None, :] <= slots[:, None, None, None]
    probs = jax.nn.softmax(jnp.where(valid, scores, -jnp.inf), axis=-1).astype(jnp.bfloat16)
    return jnp.einsum('bkgl,blkd->bkgd', probs, vals, preferred_element_type=jnp.float32).astype(jnp.bfloat16)


def solution(mesh):
    row_count = mesh.shape['row']
    hidden_spec = P('rep', 'row')
    index_spec = P(('rep', 'row'))
    cache_spec = P(None, ('rep', 'row'), None, 'col', None)
    gain_spec = P(None, 'row')
    weight_spec = P(None, 'row', 'col')

    def rms_norm(hidden, gain):
        hidden_f = hidden.astype(jnp.float32)
        square_sum = lax.psum(jnp.sum(hidden_f * hidden_f, axis=-1, keepdims=True), 'row')
        scale = lax.rsqrt(square_sum / (hidden.shape[-1] * row_count) + EPS)
        return (hidden_f * scale * gain.astype(jnp.float32)).astype(jnp.bfloat16)

    def sum_rows(partial):
        return lax.psum_scatter(partial.astype(jnp.bfloat16), 'row', scatter_dimension=0, tiled=True)

    def to_row_features(block):
        whole = lax.all_gather(block, 'col', axis=1, tiled=True)
        return lax.all_to_all(whole, 'row', 1, 0, tiled=True)

    def decoder_layer(hidden, layer, cache_k, cache_v, positions, slots, weights):
        norm_attn, norm_mlp, w_query, w_key, w_value, w_out, w_gate, w_up, w_down = weights
        head_dim = cache_k.shape[-1]
        kv_local = cache_k.shape[-2]
        q_local = w_query.shape[-1]
        kv_cols = w_key.shape[-1]
        ff_local = w_gate.shape[-1]
        normed = rms_norm(hidden, norm_attn[layer])
        qkv_part = jnp.concatenate([
            jnp.dot(normed, w_query[layer], preferred_element_type=jnp.float32),
            jnp.dot(normed, w_key[layer], preferred_element_type=jnp.float32),
            jnp.dot(normed, w_value[layer], preferred_element_type=jnp.float32)], axis=1)
        qkv_local = sum_rows(qkv_part)
        batch_local = qkv_local.shape[0]
        query = rope_rotate(qkv_local[:, :q_local].reshape(batch_local, -1, head_dim), positions)
        key_new = rope_rotate(qkv_local[:, q_local:q_local + kv_cols].reshape(batch_local, kv_local, head_dim), positions)
        value_new = qkv_local[:, q_local + kv_cols:].reshape(batch_local, kv_local, head_dim)
        rows = jnp.arange(batch_local)
        cache_k = cache_k.at[layer, rows, slots].set(key_new)
        cache_v = cache_v.at[layer, rows, slots].set(value_new)
        attended = attend_local(query.reshape(batch_local, kv_local, -1, head_dim), cache_k[layer], cache_v[layer], slots)
        attn_rows = to_row_features(attended.reshape(batch_local, -1))
        attn_out = to_row_features(sum_rows(jnp.dot(attn_rows, w_out[layer], preferred_element_type=jnp.float32)))
        hidden = add_residual(hidden, attn_out)
        normed = rms_norm(hidden, norm_mlp[layer])
        gate_up = sum_rows(jnp.concatenate([
            jnp.dot(normed, w_gate[layer], preferred_element_type=jnp.float32),
            jnp.dot(normed, w_up[layer], preferred_element_type=jnp.float32)], axis=1))
        activated = (jax.nn.silu(gate_up[:, :ff_local].astype(jnp.float32)) * gate_up[:, ff_local:].astype(jnp.float32)).astype(jnp.bfloat16)
        down_out = to_row_features(sum_rows(jnp.dot(to_row_features(activated), w_down[layer], preferred_element_type=jnp.float32)))
        return add_residual(hidden, down_out), cache_k, cache_v

    def device_program(hidden_0, hidden_1, positions, lengths, cache_k, cache_v, norm_attn, norm_mlp, w_query, w_key, w_value, w_out, w_gate, w_up, w_down):
        weights = (norm_attn, norm_mlp, w_query, w_key, w_value, w_out, w_gate, w_up, w_down)
        outputs = []
        for step, hidden in enumerate((hidden_0, hidden_1)):
            for layer in range(w_query.shape[0]):
                hidden, cache_k, cache_v = decoder_layer(hidden, layer, cache_k, cache_v, positions + step, lengths + step, weights)
            outputs.append(hidden)
        return outputs[0], outputs[1], cache_k, cache_v

    return jax.shard_map(device_program, mesh=mesh,
                         in_specs=(hidden_spec, hidden_spec, index_spec, index_spec, cache_spec, cache_spec, gain_spec, gain_spec) + (weight_spec,) * 7,
                         out_specs=(hidden_spec, hidden_spec, cache_spec, cache_spec), check_vma=False)
```

profile of v0, /device:TPU:0, one launch (start us, length us, event | category | flops | bytes accessed | tf_op | source)
XLA Modules:
  0.0 758.4 jit_solution(2568190418662677380)
XLA Ops:
  9.5 8.7 %psum.56 = f32[16,1]{0,1:T(1,128)S(1)} all-reduce(f32[16,1]{0,1:T(1,128)S(1)} %bitcast.333), channel_id=1, replica_groups=mesh['rep'=1,'col'=2,'row'=4] {'row'}, use_global_device_ids=true, to_apply=%region_1.0 | all-reduce | flops 16 | bytes 128 | tf_op jit(solution)/shard_map/psum | solution.py:44
  22.6 5.1 fusion.88
  32.6 22.2 %all-reduce.35.cloned.1.call-done = bf16[16,4096]{1,0:T(8,128)(2,1)} async-done(((bf16[16,4096]{1,0:T(8,128)(2,1)}), bf16[16,4096]{1,0:T(8,128)(2,1)}) %all-reduce.35.cloned.1.call-update) | async-done | bytes 131088
  59.5 4.5 all_gather.48
  64.0 6.4 all_to_all.256
  70.4 5.7 fusion.94
  76.1 26.2 %all-reduce.37.cloned.1.call-done = bf16[16,3072]{1,0:T(8,128)(2,1)} async-done(((bf16[16,3072]{1,0:T(8,128)(2,1)}), bf16[16,3072]{1,0:T(8,128)(2,1)}) %all-reduce.37.cloned.1.call-update) | async-done | bytes 98320
  103.1 4.5 all_gather.49
  114.9 5.8 psum.57
  120.6 10.0 %fusion.62 = bf16[16,8192]{1,0:T(8,128)(2,1)S(1)} fusion(bf16[2,1536,8192]{2,1,0:T(8,128)(2,1)} %param.28, bf16[16,1536]{1,0:T(8,128)(2,1)S(1)} %get-tuple-element.35, f32[1536]{0:T(1024)S(1)} %get-tuple-element.9, f32[16]{0:T(128)S(1)} %rsqrt_bitcast_fusion.6), kind=kOutput, calls=%fused_computation.66 | convolution fusion | flops 402882560 | bytes 25483328 | tf_op jit(solution)/shard_map/dot_general | solution.py:82
  130.6 10.0 %fusion.56 = bf16[16,8192]{1,0:T(8,128)(2,1)S(1)} fusion(bf16[2,1536,8192]{2,1,0:T(8,128)(2,1)} %param.27, bf16[16,1536]{1,0:T(8,128)(2,1)S(1)} %get-tuple-element.35, f32[1536]{0:T(1024)S(1)} %get-tuple-element.9, f32[16]{0:T(128)S(1)} %rsqrt_bitcast_fusion.6), kind=kOutput, calls=%fused_computation.64 | convolution fusion | flops 402882560 | bytes 25483328 | tf_op jit(solution)/shard_map/dot_general | solution.py:81
  141.5 28.5 %all-reduce.39.cloned.1.call-done = bf16[16,16384]{1,0:T(8,128)(2,1)} async-done(((bf16[16,16384]{1,0:T(8,128)(2,1)}), bf16[16,16384]{1,0:T(8,128)(2,1)}) %all-reduce.39.cloned.1.call-update) | async-done | bytes 524304
  171.1 4.9 all_gather.50
  176.1 7.0 all_to_all.257
  183.1 10.6 %fusion.112 = bf16[16,3072]{1,0:T(8,128)(2,1)} fusion(bf16[16,4096]{1,0:T(8,128)(2,1)S(1)} %all_to_all.201, bf16[2,4096,3072]{2,1,0:T(8,128)(2,1)} %param.29), kind=kOutput, calls=%fused_computation.88 | convolution fusion | flops 402702336 | bytes 25395200 | tf_op jit(solution)/shard_map/dot_general | solution.py:84
  193.7 26.2 %all-reduce.41.cloned.1.call-done = bf16[16,3072]{1,0:T(8,128)(2,1)} async-done(((bf16[16,3072]{1,0:T(8,128)(2,1)}), bf16[16,3072]{1,0:T(8,128)(2,1)}) %all-reduce.41.cloned.1.call-update) | async-done | bytes 98320
  220.7 4.5 all_gather.51
  228.7 3.6 all-to-all-done.3
  232.5 5.9 all-reduce.17
  245.5 5.1 fusion.91
  250.6 5.1 fusion.100
  257.1 27.4 %all-reduce.57.cloned.1.call-done = (bf16[16,4096]{1,0:T(8,128)(2,1)}, bf16[16,4096]{1,0:T(8,128)(2,1)}) async-done(((bf16[16,4096]{1,0:T(8,128)(2,1)}, bf16[16,4096]{1,0:T(8,128)(2,1)}), (bf16[16,4096]{1,0:T(8,128)(2,1)}, bf16[16,4096]{1,0:T(8,128)(2,1)})) %all-reduce.57.cloned.1.call-update) | async-done | bytes 262160
  292.9 4.5 all_gather.56
  297.4 6.4 all_to_all.258
  303.8 5.7 fusion.97
  309.5 26.2 %all-reduce.43.cloned.1.call-done = bf16[16,3072]{1,0:T(8,128)(2,1)} async-done(((bf16[16,3072]{1,0:T(8,128)(2,1)}), bf16[16,3072]{1,0:T(8,128)(2,1)}) %all-reduce.43.cloned.1.call-update) | async-done | bytes 98320
  336.5 4.5 all_gather.57
  341.0 6.4 all_to_all.259
  347.6 5.8 psum.61
  353.3 10.0 %fusion.65 = bf16[16,8192]{1,0:T(8,128)(2,1)S(1)} fusion(bf16[2,1536,8192]{2,1,0:T(8,128)(2,1)} %param.28, bf16[16,1536]{1,0:T(8,128)(2,1)S(1)} %get-tuple-element.31, f32[16]{0:T(128)S(1)} %rsqrt_bitcast_fusion.2, f32[1536]{0:T(1024)} %copy-done.7), kind=kOutput, calls=%fused_computation.67 | convolution fusion | flops 402882560 | bytes 25485376 | tf_op jit(solution)/shard_map/dot_general | solution.py:82
  363.4 10.0 %fusion.59 = bf16[16,8192]{1,0:T(8,128)(2,1)S(1)} fusion(bf16[2,1536,8192]{2,1,0:T(8,128)(2,1)} %param.27, bf16[16,1536]{1,0:T(8,128)(2,1)S(1)} %get-tuple-element.31, f32[16]{0:T(128)S(1)} %rsqrt_bitcast_fusion.2, f32[1536]{0:T(1024)S(1)} %copy-done.8), kind=kOutput, calls=%fused_computation.65 | convolution fusion | flops 402882560 | bytes 25483328 | tf_op jit(solution)/shard_map/dot_general | solution.py:81
  375.0 27.7 %all-reduce.45.cloned.1.call-done = bf16[16,16384]{1,0:T(8,128)(2,1)} async-done(((bf16[16,16384]{1,0:T(8,128)(2,1)}), bf16[16,16384]{1,0:T(8,128)(2,1)}) %all-reduce.45.cloned.1.call-update) | async-done | bytes 524304
  403.9 4.9 all_gather.58
  412.5 4.0 all-to-all-done.10
  417.2 10.6 %fusion.115 = bf16[16,3072]{1,0:T(8,128)(2,1)} fusion(bf16[16,4096]{1,0:T(8,128)(2,1)} %all_to_all.225, bf16[2,4096,3072]{2,1,0:T(8,128)(2,1)} %param.29), kind=kOutput, calls=%fused_computation.89 | convolution fusion | flops 402702336 | bytes 25395200 | tf_op jit(solution)/shard_map/dot_general | solution.py:84
  428.2 25.8 %all-reduce.47.cloned.1.call-done = bf16[16,3072]{1,0:T(8,128)(2,1)} async-done(((bf16[16,3072]{1,0:T(8,128)(2,1)}), bf16[16,3072]{1,0:T(8,128)(2,1)}) %all-reduce.47.cloned.1.call-update) | async-done | bytes 98320
  454.8 4.5 all_gather.59
  462.8 3.6 all-to-all-done.11
  466.6 5.8 psum.62
  475.9 5.1 fusion.103
  482.0 4.5 all_gather.52
  486.5 6.4 all_to_all.260
  492.9 15.7 %all-reduce.49.cloned.1.call-done = bf16[16,4096]{1,0:T(8,128)(2,1)} async-done(((bf16[16,4096]{1,0:T(8,128)(2,1)}), bf16[16,4096]{1,0:T(8,128)(2,1)}) %all-reduce.49.cloned.1.call-update) | async-done | bytes 131088
  513.3 4.5 all_gather.60
  521.1 5.7 fusion.106
  526.8 5.7 fusion.109
  532.5 28.0 %all-reduce.55.cloned.1.call-done = (bf16[16,3072]{1,0:T(8,128)(2,1)}, bf16[16,3072]{1,0:T(8,128)(2,1)}) async-done(((bf16[16,3072]{1,0:T(8,128)(2,1)}, bf16[16,3072]{1,0:T(8,128)(2,1)}), (bf16[16,3072]{1,0:T(8,128)(2,1)}, bf16[16,3072]{1,0:T(8,128)(2,1)})) %all-reduce.55.cloned.1.call-update) | async-done | bytes 196624
  561.4 4.5 all_gather.61
  570.0 4.5 all_gather.53
  578.0 3.6 all-to-all-done.5
  581.7 6.0 all-reduce.16
  587.7 10.0 %fusion.77 = bf16[16,8192]{1,0:T(8,128)(2,1)S(1)} fusion(bf16[2,1536,8192]{2,1,0:T(8,128)(2,1)} %param.28, bf16[16,1536]{1,0:T(8,128)(2,1)S(1)} %get-tuple-element.25, f32[16]{0:T(128)S(1)} %rsqrt_bitcast_fusion, f32[1536]{0:T(1024)S(1)} %copy-done.6), kind=kOutput, calls=%fused_computation.71 | convolution fusion | flops 402882560 | bytes 25483328 | tf_op jit(solution)/shard_map/dot_general | solution.py:82
  597.8 10.0 %fusion.71 = bf16[16,8192]{1,0:T(8,128)(2,1)S(1)} fusion(bf16[2,1536,8192]{2,1,0:T(8,128)(2,1)} %param.27, bf16[16,1536]{1,0:T(8,128)(2,1)S(1)} %get-tuple-element.25, f32[16]{0:T(128)S(1)} %rsqrt_bitcast_fusion, f32[1536]{0:T(1024)S(1)} %copy-done.6), kind=kOutput, calls=%fused_computation.69 | convolution fusion | flops 402882560 | bytes 25483328 | tf_op jit(solution)/shard_map/dot_general | solution.py:81
  607.8 10.0 %fusion.74 = bf16[16,8192]{1,0:T(8,128)(2,1)S(1)} fusion(bf16[2,1536,8192]{2,1,0:T(8,128)(2,1)} %param.28, bf16[16,1536]{1,0:T(8,128)(2,1)S(1)} %get-tuple-element.27, f32[1536]{0:T(1024)S(1)} %copy-done.6, f32[16]{0:T(128)S(1)} %rsqrt_bitcast_fusion.4), kind=kOutput, calls=%fused_computation.70 | convolution fusion | flops 402882560 | bytes 25483328 | tf_op jit(solution)/shard_map/dot_general | solution.py:82
  617.8 10.0 %fusion.68 = bf16[16,8192]{1,0:T(8,128)(2,1)S(1)} fusion(bf16[2,1536,8192]{2,1,0:T(8,128)(2,1)} %param.27, bf16[16,1536]{1,0:T(8,128)(2,1)S(1)} %get-tuple-element.27, f32[1536]{0:T(1024)S(1)} %copy-done.6, f32[16]{0:T(128)S(1)} %rsqrt_bitcast_fusion.4), kind=kOutput, calls=%fused_computation.68 | convolution fusion | flops 402882560 | bytes 25483328 | tf_op jit(solution)/shard_map/dot_general | solution.py:81
  629.5 31.7 %all-reduce.53.cloned.1.call-done = (bf16[16,16384]{1,0:T(8,128)(2,1)}, bf16[16,16384]{1,0:T(8,128)(2,1)}) async-done(((bf16[16,16384]{1,0:T(8,128)(2,1)}, bf16[16,16384]{1,0:T(8,128)(2,1)}), (bf16[16,16384]{1,0:T(8,128)(2,1)}, bf16[16,16384]{1,0:T(8,128)(2,1)})) %all-reduce.53.cloned.1.call-update) | async-done | bytes 1048592
  662.3 4.9 all_gather.62
  671.7 5.1 all_gather.54
  676.8 3.3 all-to-all-start.6
  680.2 10.5 %fusion.121 = bf16[16,3072]{1,0:T(8,128)(2,1)} fusion(bf16[16,4096]{1,0:T(8,128)(2,1)S(1)} %all_to_all.237, bf16[2,4096,3072]{2,1,0:T(8,128)(2,1)} %param.29), kind=kOutput, calls=%fused_computation.91 | convolution fusion | flops 402702336 | bytes 25395200 | tf_op jit(solution)/shard_map/dot_general | solution.py:84
  690.8 10.6 %fusion.118 = bf16[16,3072]{1,0:T(8,128)(2,1)} fusion(bf16[16,4096]{1,0:T(8,128)(2,1)S(1)} %all_to_all.213, bf16[2,4096,3072]{2,1,0:T(8,128)(2,1)} %param.29), kind=kOutput, calls=%fused_computation.90 | convolution fusion | flops 402702336 | bytes 25395200 | tf_op jit(solution)/shard_map/dot_general | solution.py:84
  701.4 28.0 %all-reduce.51.cloned.1.call-done = (bf16[16,3072]{1,0:T(8,128)(2,1)}, bf16[16,3072]{1,0:T(8,128)(2,1)}) async-done(((bf16[16,3072]{1,0:T(8,128)(2,1)}, bf16[16,3072]{1,0:T(8,128)(2,1)}), (bf16[16,3072]{1,0:T(8,128)(2,1)}, bf16[16,3072]{1,0:T(8,128)(2,1)})) %all-reduce.51.cloned.1.call-update) | async-done | bytes 196624
  730.2 4.5 all_gather.55
  738.8 4.5 all_gather.63
  (213 shorter events, 101.3 us)
Async XLA Ops:
  7.2 107.6 %copy-start.3 = (bf16[16,1536]{1,0:T(8,128)(2,1)S(1)}, bf16[16,1536]{1,0:T(8,128)(2,1)}, u32[]{:S(2)}) copy-start(bf16[16,1536]{1,0:T(8,128)(2,1)} %param.15) | copy-start | bytes 147460
  7.2 51.1 %copy-start.1 = (bf16[2,4,128,4,128]{4,3,2,1,0:T(4,128)(2,1)S(1)}, bf16[2,4,128,4,128]{4,3,2,1,0:T(4,128)(2,1)}, u32[]{:S(2)}) copy-start(bf16[2,4,128,4,128]{4,3,2,1,0:T(4,128)(2,1)} %param.20) | copy-start | bytes 3145732
  7.2 103.8 %copy-start.5 = (bf16[2,1536]{1,0:T(2,128)(2,1)S(1)}, bf16[2,1536]{1,0:T(2,128)(2,1)}, u32[]{:S(2)}) copy-start(bf16[2,1536]{1,0:T(2,128)(2,1)} %param.22) | copy-start | bytes 18436
  7.2 47.6 %all-reduce.35.cloned.1.call-start = ((), (), s32[]{:S(2)}) async-start(), calls=%async_computation.16 | async-start | bytes 262144
  28.4 73.9 %all-reduce.37.cloned.1.call-start = ((), (), s32[]{:S(2)}) async-start(), calls=%async_computation.17 | async-start | bytes 196608
  107.6 7.1 all-to-all-start.1
  110.9 59.1 %all-reduce.39.cloned.1.call-start = ((), (), s32[]{:S(2)}) async-start(), calls=%async_computation.18 | async-start | bytes 1048576
  111.6 29.0 %copy-start.7 = (f32[1536]{0:T(1024)}, f32[1536]{0:T(1024)S(1)}, u32[]{:S(2)}) copy-start(f32[1536]{0:T(1024)S(1)} %get-tuple-element.9) | copy-start | bytes 18436
  141.5 78.4 %all-reduce.41.cloned.1.call-start = ((), (), s32[]{:S(2)}) async-start(), calls=%async_computation.19 | async-start | bytes 196608
  183.1 10.6 %copy-start.11 = (s32[4]{0:T(128)S(1)}, s32[4]{0:T(128)}, u32[]{:S(2)}) copy-start(s32[4]{0:T(128)} %param.18) | copy-start | bytes 52
  183.1 45.4 %copy-start.4 = (bf16[16,1536]{1,0:T(8,128)(2,1)S(1)}, bf16[16,1536]{1,0:T(8,128)(2,1)}, u32[]{:S(2)}) copy-start(bf16[16,1536]{1,0:T(8,128)(2,1)} %param.16) | copy-start | bytes 147460
  225.2 7.1 all-to-all-start.3
  228.5 56.0 %all-reduce.57.cloned.1.call-start = ((), (), s32[]{:S(2)}) async-start(), calls=%async_computation.27 | async-start | bytes 524288
  257.0 78.7 %all-reduce.43.cloned.1.call-start = ((), (), s32[]{:S(2)}) async-start(), calls=%async_computation.20 | async-start | bytes 196608
  257.1 33.4 %copy-start.9 = (pred[4,128]{1,0:T(4,128)(4,1)}, pred[4,128]{1,0:T(4,128)(4,1)S(1)}, u32[]{:S(2)}) copy-start(pred[4,128]{1,0:T(4,128)(4,1)S(1)} %iota_compare_fusion) | copy-start | bytes 1540
  309.5 53.9 %copy-start.8 = (f32[1536]{0:T(1024)S(1)}, f32[1536]{0:T(1024)}, u32[]{:S(2)}) copy-start(f32[1536]{0:T(1024)} %copy-done.7) | copy-start | bytes 18436
  309.5 93.3 %all-reduce.45.cloned.1.call-start = ((), (), s32[]{:S(2)}) async-start(), calls=%async_computation.21 | async-start | bytes 1048576
  408.8 7.7 %all-to-all-start.10 = ((bf16[4,4,4096]{2,0,1:T(4,128)(2,1)}), bf16[4,4,4096]{2,0,1:T(4,128)(2,1)S(1)}, u32[]{:S(2)}, u32[]{:S(2)}) async-start(bf16[4,4,4096]{2,0,1:T(4,128)(2,1)} %bitcast.69), calls=%async_computation.10 | async-start | bytes 262144 | tf_op jit(solution)/shard_map/all_to_all | solution.py:53
  412.1 41.8 %all-reduce.47.cloned.1.call-start = ((), (), s32[]{:S(2)}) async-start(), calls=%async_computation.22 | async-start | bytes 196608
  417.2 95.1 %copy-start.10 = (pred[4,128]{1,0:T(4,128)(4,1)S(1)}, pred[4,128]{1,0:T(4,128)(4,1)}, u32[]{:S(2)}) copy-start(pred[4,128]{1,0:T(4,128)(4,1)} %copy-done.9) | copy-start | bytes 1540
  459.3 7.1 all-to-all-start.11
  462.6 46.0 %all-reduce.49.cloned.1.call-start = ((), (), s32[]{:S(2)}) async-start(), calls=%async_computation.23 | async-start | bytes 262144
  474.1 113.7 %copy-start.6 = (f32[1536]{0:T(1024)S(1)}, f32[1536]{0:T(1024)}, u32[]{:S(2)}) copy-start(f32[1536]{0:T(1024)} %get-tuple-element.8) | copy-start | bytes 18436
  511.2 86.5 %copy-start.2 = (bf16[2,4,128,4,128]{4,3,2,1,0:T(4,128)(2,1)}, bf16[2,4,128,4,128]{4,3,2,1,0:T(4,128)(2,1)S(1)}, u32[]{:S(2)}) copy-start(bf16[2,4,128,4,128]{4,3,2,1,0:T(4,128)(2,1)S(1)} %scatter_fusion.6) | copy-start | bytes 3145732
  511.9 85.9 %copy-start = (bf16[2,4,128,4,128]{4,3,2,1,0:T(4,128)(2,1)}, bf16[2,4,128,4,128]{4,3,2,1,0:T(4,128)(2,1)S(1)}, u32[]{:S(2)}) copy-start(bf16[2,4,128,4,128]{4,3,2,1,0:T(4,128)(2,1)S(1)} %scatter_fusion.7) | copy-start | bytes 3145732
  517.8 9.0 %all-to-all-start.12 = ((bf16[4,4,1536]{2,0,1:T(4,128)(2,1)}), bf16[4,4,1536]{2,0,1:T(4,128)(2,1)S(1)}, u32[]{:S(2)}, u32[]{:S(2)}) async-start(bf16[4,4,1536]{2,0,1:T(4,128)(2,1)} %bitcast.82), calls=%async_computation.12 | async-start | bytes 98304 | tf_op jit(solution)/shard_map/all_to_all | solution.py:53
  521.1 39.5 %all-reduce.55.cloned.1.call-start = ((), (), s32[]{:S(2)}) async-start(), calls=%async_computation.26 | async-start | bytes 393216
  565.9 8.6 %all-to-all-start.13 = ((bf16[4,4,1536]{2,0,1:T(4,128)(2,1)}), bf16[4,4,1536]{2,0,1:T(4,128)(2,1)S(1)}, u32[]{:S(2)}, u32[]{:S(2)}) async-start(bf16[4,4,1536]{2,0,1:T(4,128)(2,1)} %bitcast.84), calls=%async_computation.13 | async-start | bytes 98304 | tf_op jit(solution)/shard_map/all_to_all | solution.py:53
  574.5 7.1 all-to-all-start.5
  577.7 83.4 %all-reduce.53.cloned.1.call-start = ((), (), s32[]{:S(2)}) async-start(), calls=%async_computation.25 | async-start | bytes 2097152
  667.2 9.6 %all-to-all-start.14 = ((bf16[4,4,4096]{2,0,1:T(4,128)(2,1)}), bf16[4,4,4096]{2,0,1:T(4,128)(2,1)S(1)}, u32[]{:S(2)}, u32[]{:S(2)}) async-start(bf16[4,4,4096]{2,0,1:T(4,128)(2,1)} %bitcast.88), calls=%async_computation.14 | async-start | bytes 262144 | tf_op jit(solution)/shard_map/all_to_all | solution.py:53
  676.8 14.0 %all-to-all-start.6 = ((bf16[4,4,4096]{2,0,1:T(4,128)(2,1)}), bf16[4,4,4096]{2,0,1:T(4,128)(2,1)S(1)}, u32[]{:S(2)}, u32[]{:S(2)}) async-start(bf16[4,4,4096]{2,0,1:T(4,128)(2,1)} %bitcast.48), calls=%async_computation.6 | async-start | bytes 262144 | tf_op jit(solution)/shard_map/all_to_all | solution.py:53
  680.1 49.3 %all-reduce.51.cloned.1.call-start = ((), (), s32[]{:S(2)}) async-start(), calls=%async_computation.24 | async-start | bytes 393216
  734.7 8.6 %all-to-all-start.7 = ((bf16[4,4,1536]{2,0,1:T(4,128)(2,1)}), bf16[4,4,1536]{2,0,1:T(4,128)(2,1)S(1)}, u32[]{:S(2)}, u32[]{:S(2)}) async-start(bf16[4,4,1536]{2,0,1:T(4,128)(2,1)} %bitcast.51), calls=%async_computation.7 | async-start | bytes 98304 | tf_op jit(solution)/shard_map/all_to_all | solution.py:53
  743.3 7.1 all-to-all-start.15
Sparse Core Ops, SparseCore 0:
  28.5 26.2 all-reduce.34
  76.2 26.0 all-reduce.36
  141.6 28.3 all-reduce.38
  193.8 26.0 all-reduce.40
  257.1 27.3 all-reduce.56
  309.6 26.0 all-reduce.42
  374.3 28.3 all-reduce.44
  427.9 26.0 all-reduce.46
  481.7 26.7 all-reduce.48
  532.6 27.8 all-reduce.54
  629.6 31.5 all-reduce.52
  701.5 27.8 all-reduce.50
where the time goes:
time: 770 us; the launch traced here: 758 us
  waiting for transfers between devices  335 us (44%)
  matrix products  183 us (24%)
  blocking collectives  144 us (19%)
  starting transfers between devices  36.9 us (5%)
  other arithmetic  25.1 us (3%)
  local copies, waits for them, and re-layouts  18.1 us (2%)
  between operations  16.1 us (2%)
    unnamed x24, waiting for transfers between devices  314 us
    all_gather x16, blocking collectives, to_row_features(): whole = lax.all_gather(block, 'col', axis=1, tiled=True)  73.9 us
    dot_general x4, matrix products, decoder_layer(): jnp.dot(to_row_features(activated), w_down[layer], preferred_element_type...  42.2 us
    dot_general x4, matrix products, decoder_layer(): jnp.dot(normed, w_up[layer], preferred_element_type=jnp.float32)  39.9 us
    dot_general x4, matrix products, decoder_layer(): jnp.dot(normed, w_gate[layer], preferred_element_type=jnp.float32)  39.9 us
    psum x6, blocking collectives, rms_norm(): lax.psum(jnp.sum(hidden_f * hidden_f, axis=-1, keepdims=True), 'row')  37.9 us
    all_to_all x11, starting transfers between devices, to_row_features(): return lax.all_to_all(whole, 'row', 1, 0, tiled=True)  36.2 us
    all_to_all x5, blocking collectives, to_row_features(): return lax.all_to_all(whole, 'row', 1, 0, tiled=True)  32.5 us
  transfers between devices with their start and end apart: 23, of which 18 were waited for; matrix products, arithmetic and copies ran while one was open for 3% of the time, Pallas kernels for 0%

commit v1 on v0

v1 whole, which is shorter than its diff:
```python
import functools

import jax
import jax.numpy as jnp
from jax import lax
from jax.experimental import pallas as pl
from jax.experimental.pallas import tpu as pltpu
from jax.sharding import PartitionSpec as P

ROPE_BASE = 1000000.0
EPS = 1e-05
MESH = pl.DeviceIdType.MESH
F32 = jnp.float32
BF16 = jnp.bfloat16

LAYERS = 2
ROWS = 4
COLS = 2
SEQS = 4
RB = 8
D = 1536
HD = 128
QH = 24
KVH = 4
QW = QH * HD
KVW = KVH * HD
FF = 8192
FK = 4096
WIDTH = 6144
CTX = 128
CW = 512
KD = 1024
NS = 30

QKV_N = QW + 2 * KVW
KINDS = ['k', 'v'] + ['q'] * 6 + ['o'] * 6 + ['g', 'u'] * 16 + ['d'] * 24
INDEX = [0, 0] + list(range(6)) + list(range(6)) + [i // 2 for i in range(32)] + list(range(24))
PER_LAYER = len(KINDS)
TOTAL = LAYERS * PER_LAYER
BASE = {'qkv': 0, 'o': 8, 'gu': 14, 'd': 46}


def chunk_of(seq):
    if seq >= TOTAL:
        return None
    layer, pos = divmod(seq, PER_LAYER)
    return layer, KINDS[pos], INDEX[pos]


def mega_kernel(h0, h1, positions, lengths, ck, cv, na, nm, wq, wk, wv, wo, wg, wu, wd,
                out0, out1, kout, vout,
                wbuf, kbuf, vbuf, hbuf, gabuf, gmbuf, nbuf, abuf, xown,
                q_scr, kn_scr, vn_scr, o_scr, lim_scr, cos_scr, sin_scr,
                is_send, is_recv, xi_send, xi_recv,
                qkv_s, qkv_r, o_s, o_r, gu_s, gu_r, d_s, d_r,
                ao_s, ao_r, x_s, x_r, aa_s, aa_r, st_s, st_r,
                wsem, lsem, csem, isem, xisem, rssem, rrsem, assem, arsem, stsem):
    c = lax.axis_index('col')
    r = lax.axis_index('row')
    rep = lax.axis_index('rep')
    me = c * ROWS + r
    home = c == r // 2

    def dev(cc, rr):
        return (rep, cc, rr)

    small = [pltpu.make_async_copy(h0, hbuf.at[0], lsem.at[0]),
             pltpu.make_async_copy(h1, hbuf.at[1], lsem.at[1]),
             pltpu.make_async_copy(na, gabuf, lsem.at[2]),
             pltpu.make_async_copy(nm, gmbuf, lsem.at[3]),
             pltpu.make_async_copy(ck, kbuf, lsem.at[4]),
             pltpu.make_async_copy(cv, vbuf, lsem.at[5])]
    for copy in small[:4]:
        copy.start()

    def weight_copy(layer, kind, idx, slot):
        if kind == 'd':
            n, k = idx // 4, idx % 4
            src = wd.at[layer, pl.ds(pl.multiple_of(k * KD, KD), KD), pl.ds(pl.multiple_of(n * CW, CW), CW)]
            return pltpu.make_async_copy(src, wbuf.at[slot, pl.ds(0, KD)], wsem.at[slot])
        ref = {'k': wk, 'v': wv, 'q': wq, 'o': wo, 'g': wg, 'u': wu}[kind]
        src = ref.at[layer, :, pl.ds(pl.multiple_of(idx * CW, CW), CW)]
        return pltpu.make_async_copy(src, wbuf.at[slot], wsem.at[slot])

    def weight_wait(down, slot):
        if down:
            pltpu.make_async_copy(wd.at[0, pl.ds(0, KD), pl.ds(0, CW)], wbuf.at[slot, pl.ds(0, KD)], wsem.at[slot]).wait()
        else:
            pltpu.make_async_copy(wq.at[0, :, pl.ds(0, CW)], wbuf.at[slot], wsem.at[slot]).wait()

    def issue_initial(lo, hi):
        seq = lo
        while seq < hi:
            layer, kind, idx = chunk_of(seq)
            weight_copy(layer, kind, idx, seq % NS).start()
            seq += 1

    issue_initial(0, 8)
    for copy in small[4:]:
        copy.start()
    issue_initial(8, NS)

    def run_phase(layer, base, iters, per, down, body):
        start = layer * PER_LAYER + base

        def future(t):
            return [chunk_of(start + t * per + e + NS) for e in range(per)]

        def signature(t):
            return [None if f is None else f[:2] for f in future(t)]

        t = 0
        while t < iters:
            end = t + 1
            while end < iters and signature(end) == signature(t):
                end += 1
            first = future(t)
            step = [0] * per
            if end - t > 1:
                nxt = future(t + 1)
                step = [0 if f is None else g[2] - f[2] for f, g in zip(first, nxt)]
                for tt in range(t, end):
                    for f, s, g in zip(first, step, future(tt)):
                        assert f is None or f[2] + s * (tt - t) == g[2]

            def one(i, carry, t=t, first=first, step=step):
                slots = [lax.rem(start + i * per + e, NS) for e in range(per)]
                for s in slots:
                    weight_wait(down, s)
                body(i, slots)
                for f, st, s in zip(first, step, slots):
                    if f is not None:
                        weight_copy(f[0], f[1], f[2] + st * (i - t), s).start()
                return carry

            if end - t == 1:
                one(t, 0)
            else:
                lax.fori_loop(t, end, one, 0)
            t = end

    def rs_send(send, recv, ssem, rsem, off, value):
        width = value.shape[1]
        cols = pl.ds(pl.multiple_of(off, width), width)
        for p in range(ROWS):
            send[p, :, cols] = value[p * RB:(p + 1) * RB].astype(BF16)
        for d in (2, 3, 1):
            tgt = lax.rem(r + d, ROWS)
            pltpu.make_async_remote_copy(send.at[tgt, :, cols], recv.at[d - 1, :, cols], ssem, rsem,
                                         device_id=dev(c, tgt), device_id_type=MESH).start()

    def rs_wait_recv(recv, ssem, rsem):
        pltpu.make_async_remote_copy(recv, recv, ssem, rsem, device_id=dev(c, r), device_id_type=MESH).wait_recv()

    def rs_wait_send(send, ssem, rsem):
        ref = send.at[pl.ds(0, 3)]
        pltpu.make_async_remote_copy(ref, ref, ssem, rsem, device_id=dev(c, r), device_id_type=MESH).wait_send()

    def rs_sum(send, recv, lo, hi):
        acc = send[r, :, lo:hi].astype(F32)
        for d in range(ROWS - 1):
            acc = acc + recv[d, :, lo:hi].astype(F32)
        return acc

    def a2a_copy(send, recv, ssem, rsem, j, cc):
        return pltpu.make_async_remote_copy(send.at[j], recv.at[r], ssem.at[j * COLS + cc], rsem.at[r],
                                            device_id=dev(cc, 2 * c + j), device_id_type=MESH)

    def a2a_self(j, cc):
        return jnp.logical_and(c == cc, r == 2 * c + j)

    def a2a_send(send, recv, ssem, rsem, j):
        for cc in range(COLS):
            mine = a2a_self(j, cc)

            @pl.when(jnp.logical_not(mine))
            def _():
                a2a_copy(send, recv, ssem, rsem, j, cc).start()

            @pl.when(mine)
            def _():
                recv[r] = send[j]

    def a2a_wait_recv(send, recv, ssem, rsem):
        for s in range(ROWS):
            @pl.when(jnp.logical_not(jnp.logical_and(home, r == s)))
            def _():
                pltpu.make_async_remote_copy(send.at[0], recv.at[s], ssem.at[0], rsem.at[s],
                                             device_id=dev(c, r), device_id_type=MESH).wait_recv()

    def a2a_wait_send(send, recv, ssem, rsem):
        for j in range(2):
            for cc in range(COLS):
                @pl.when(jnp.logical_not(a2a_self(j, cc)))
                def _():
                    a2a_copy(send, recv, ssem, rsem, j, cc).wait_send()

    def stat_copy(send, recv, ssem, rsem, e):
        tgt = lax.rem(me + e, COLS * ROWS)
        return pltpu.make_async_remote_copy(send, recv.at[me], ssem, rsem,
                                            device_id=dev(tgt // ROWS, lax.rem(tgt, ROWS)), device_id_type=MESH)

    barrier = pltpu.get_barrier_semaphore()
    for e in range(1, COLS * ROWS):
        tgt = lax.rem(me + e, COLS * ROWS)
        pl.semaphore_signal(barrier, inc=1, device_id=dev(tgt // ROWS, lax.rem(tgt, ROWS)), device_id_type=MESH)
    pl.semaphore_wait(barrier, COLS * ROWS - 1)

    for copy in small[:4]:
        copy.wait()
    h0v = hbuf[0].astype(F32)
    h1v = hbuf[1].astype(F32)
    blocks = [jnp.concatenate([h0v[4 * p:4 * p + 4], h1v[4 * p:4 * p + 4]], axis=0) for p in range(ROWS)]
    for p in range(ROWS):
        sq = jnp.sum(blocks[p] * blocks[p], axis=1, keepdims=True)
        is_send[p] = jnp.broadcast_to(sq, (RB, 128))
    for d in (2, 3, 1):
        tgt = lax.rem(r + d, ROWS)
        pltpu.make_async_remote_copy(is_send, is_recv.at[d - 1], isem.at[0], isem.at[1],
                                     device_id=dev(c, tgt), device_id_type=MESH).start()
    for p in range(ROWS):
        xi_send[p] = blocks[p].astype(BF16)

    @pl.when(home)
    def _():
        for d in range(1, ROWS):
            tgt = lax.rem(r + d, ROWS)
            pltpu.make_async_remote_copy(xi_send.at[tgt], xi_recv.at[lax.rem(r, 2)], xisem.at[0], xisem.at[1 + lax.rem(r, 2)],
                                         device_id=dev(c, tgt), device_id_type=MESH).start()
        xi_recv[lax.rem(r, 2)] = xi_send[r]

    rowi = lax.broadcasted_iota(jnp.int32, (RB, HD), 0)
    lane = lax.broadcasted_iota(jnp.int32, (RB, HD), 1)
    step_id = (rowi >= SEQS).astype(jnp.int32)
    seq_id = rowi - SEQS * step_id
    pos = step_id
    for b in range(SEQS):
        pos = pos + jnp.where(seq_id == b, positions[b], 0)
    half = (lane >= HD // 2)
    freq_i = jnp.where(half, lane - HD // 2, lane).astype(F32)
    inv_freq = jnp.exp(freq_i * (-13.815510557964274 / 64.0))
    angle = pos.astype(F32) * inv_freq
    cos_scr[...] = jnp.cos(angle)
    sine = jnp.sin(angle)
    sin_scr[...] = jnp.where(half, sine, -sine)

    srow = lax.broadcasted_iota(jnp.int32, (2 * QH, CTX * KVH), 0)
    scol = lax.broadcasted_iota(jnp.int32, (2 * QH, CTX * KVH), 1)
    srow_step = (srow >= QH).astype(jnp.int32)
    srow_h = srow - QH * srow_step
    srow_kv = (srow_h >= 6).astype(jnp.int32) + (srow_h >= 12).astype(jnp.int32) + (srow_h >= 18).astype(jnp.int32)
    slot = jnp.right_shift(scol, 2)
    kv_of = jnp.bitwise_and(scol, 3)
    lim_scr[...] = jnp.where(kv_of == srow_kv, slot - srow_step, 1 << 20)

    pltpu.make_async_remote_copy(is_recv, is_recv, isem.at[0], isem.at[1], device_id=dev(c, r), device_id_type=MESH).wait_recv()

    def normalise(p, xblock, total, gain):
        scale = lax.rsqrt(total * (1.0 / WIDTH) + EPS)[:, :1]
        return xblock * scale * gain

    def put_rows(dst, parts):
        dst[...] = jnp.concatenate(parts, axis=0).astype(BF16)

    gain = gabuf[0:1, :].astype(F32)
    parts = []
    for p in range(ROWS):
        total = is_send[p] + is_recv[0, p] + is_recv[1, p] + is_recv[2, p]
        parts.append(normalise(p, blocks[p], total, gain))
    put_rows(nbuf, parts)

    for copy in small[4:]:
        copy.wait()

    out_copies = []
    for layer in range(LAYERS):
        qs, qr = qkv_s.at[layer], qkv_r.at[layer]
        qsem = (rssem.at[layer, 0], rrsem.at[layer, 0])

        def qkv_body(i, slots):
            lhs = nbuf[...]
            y = [jnp.dot(lhs, wbuf[s], preferred_element_type=F32) for s in slots]
            rs_send(qs, qr, *qsem, i * (2 * CW), jnp.concatenate(y, axis=1))

        run_phase(layer, BASE['qkv'], 4, 2, False, qkv_body)
        rs_wait_recv(qr, *qsem)

        cosv, sinv = cos_scr[...], sin_scr[...]

        def rope(block):
            value = block.astype(BF16).astype(F32)
            return (value * cosv + pltpu.roll(value, HD // 2, 1) * sinv).astype(BF16).astype(F32)

        for h in range(KVH):
            kn_scr[h * RB:(h + 1) * RB, :] = rope(rs_sum(qs, qr, h * HD, (h + 1) * HD))
            vn_scr[h * RB:(h + 1) * RB, :] = rs_sum(qs, qr, KVW + h * HD, KVW + (h + 1) * HD)
        for h in range(QH):
            q_scr[h * RB:(h + 1) * RB, :] = rope(rs_sum(qs, qr, 2 * KVW + h * HD, 2 * KVW + (h + 1) * HD))
        row_slot = jnp.right_shift(lax.broadcasted_iota(jnp.int32, (CTX * KVH, HD), 0), 2)
        for b in range(SEQS):
            length = lengths[b]

            def updated(cache, new_scr):
                value = cache[layer, b].astype(F32)
                for s in range(2):
                    new = new_scr[pl.ds(b + SEQS * s, KVH, stride=RB), :]
                    tile = jnp.concatenate([new, new], axis=0)
                    full = jnp.broadcast_to(tile[None], (CTX * KVH // 8, 8, HD)).reshape(CTX * KVH, HD)
                    value = jnp.where(row_slot == length + s, full, value)
                return value.astype(BF16)

            keys = updated(kbuf, kn_scr)
            vals = updated(vbuf, vn_scr)
            kbuf[layer, b] = keys
            vbuf[layer, b] = vals
            qb = jnp.concatenate([q_scr[pl.ds(b + SEQS * s, QH, stride=RB), :] for s in range(2)], axis=0).astype(BF16)
            scores = lax.dot_general(qb, keys, (((1,), (1,)), ((), ())), preferred_element_type=F32) * (HD ** -0.5)
            scores = jnp.where(lim_scr[...] <= length, scores, -jnp.inf)
            top = jnp.max(scores, axis=1, keepdims=True)
            e = jnp.exp(scores - top)
            probs = (e / jnp.sum(e, axis=1, keepdims=True)).astype(BF16)
            ob = jnp.dot(probs, vals, preferred_element_type=F32)
            for s in range(2):
                o_scr[pl.ds(b + SEQS * s, QH, stride=RB), :] = ob[s * QH:(s + 1) * QH]
        aos, aor = ao_s.at[layer], ao_r.at[layer]
        aosem = (assem.at[layer, 0], arsem.at[layer, 0])
        for j in range(2):
            for h in range(QH // 2):
                hh = j * (QH // 2) + h
                aos[j, :, h * HD:(h + 1) * HD] = o_scr[hh * RB:(hh + 1) * RB, :].astype(BF16)
            a2a_send(aos, aor, *aosem, j)
        for which, (buf, out) in enumerate(((kbuf, kout), (vbuf, vout))):
            copy = pltpu.make_async_copy(buf.at[layer], out.at[layer], csem.at[2 * layer + which])
            copy.start()
            out_copies.append(copy)
        a2a_wait_recv(aos, aor, *aosem)
        put_rows(nbuf, [aor[p].astype(F32) for p in range(ROWS)])

        if layer == 0:
            for j in range(2):
                @pl.when(jnp.logical_not(jnp.logical_and(home, lax.rem(r, 2) == j)))
                def _():
                    pltpu.make_async_remote_copy(xi_send.at[0], xi_recv.at[j], xisem.at[0], xisem.at[1 + j],
                                                 device_id=dev(c, r), device_id_type=MESH).wait_recv()
                xown[:, j * D:(j + 1) * D] = xi_recv[j].astype(F32)

        os_, or_ = o_s.at[layer], o_r.at[layer]
        osem = (rssem.at[layer, 1], rrsem.at[layer, 1])

        def o_body(i, slots):
            lhs = nbuf[...]
            y = [jnp.dot(lhs, wbuf[s], preferred_element_type=F32) for s in slots]
            rs_send(os_, or_, *osem, i * (2 * CW), jnp.concatenate(y, axis=1))

        def residual(send, recv, sems, which):
            rs_wait_recv(recv, *sems)
            xs, xr = x_s.at[layer, which], x_r.at[layer, which]
            xsem = (assem.at[layer, 1 + which], arsem.at[layer, 1 + which])
            squares = jnp.zeros((RB, 128), F32)
            for j in range(2):
                update = rs_sum(send, recv, j * D, (j + 1) * D).astype(BF16).astype(F32)
                x = (xown[:, j * D:(j + 1) * D] + update).astype(BF16)
                xs[j] = x
                x = x.astype(F32)
                xown[:, j * D:(j + 1) * D] = x
                a2a_send(xs, xr, *xsem, j)
                sq = x * x
                for k in range(D // 128):
                    squares = squares + sq[:, k * 128:(k + 1) * 128]
            last = layer == LAYERS - 1 and which == 1
            if not last:
                sts, stv = st_s.at[layer, which], st_r.at[layer, which]
                stat = jnp.broadcast_to(jnp.sum(squares, axis=1, keepdims=True), (RB, 128))
                sts[...] = stat
                stv[me] = stat
                for e in range(1, COLS * ROWS):
                    stat_copy(sts, stv, stsem.at[layer, which, 0], stsem.at[layer, which, 1], e).start()
            a2a_wait_recv(xs, xr, *xsem)
            if last:
                return
            seven = stv.at[pl.ds(0, COLS * ROWS - 1)]
            pltpu.make_async_remote_copy(seven, seven, stsem.at[layer, which, 0], stsem.at[layer, which, 1],
                                         device_id=dev(c, r), device_id_type=MESH).wait_recv()
            g = (gmbuf[layer:layer + 1, :] if which == 0 else gabuf[layer + 1:layer + 2, :]).astype(F32)
            parts = []
            for p in range(ROWS):
                parts.append(normalise(p, xr[p].astype(F32), stv[p] + stv[ROWS + p], g))
            put_rows(nbuf, parts)

        run_phase(layer, BASE['o'], 3, 2, False, o_body)
        residual(os_, or_, osem, 0)

        gs, gr = gu_s.at[layer], gu_r.at[layer]
        gsem = (rssem.at[layer, 2], rrsem.at[layer, 2])

        def gu_body(i, slots):
            lhs = nbuf[...]
            y = [jnp.dot(lhs, wbuf[s], preferred_element_type=F32) for s in slots]
            rs_send(gs, gr, *gsem, i * (2 * CW), jnp.concatenate(y, axis=1))

        run_phase(layer, BASE['gu'], 16, 2, False, gu_body)
        rs_wait_recv(gr, *gsem)
        aas, aar = aa_s.at[layer], aa_r.at[layer]
        aasem = (assem.at[layer, 3], arsem.at[layer, 3])
        for j in range(2):
            for i in range(8):
                lo = (j * 8 + i) * 2 * CW
                gate = rs_sum(gs, gr, lo, lo + CW).astype(BF16).astype(F32)
                up = rs_sum(gs, gr, lo + CW, lo + 2 * CW).astype(BF16).astype(F32)
                aas[j, :, i * CW:(i + 1) * CW] = (gate * jax.nn.sigmoid(gate) * up).astype(BF16)
            a2a_send(aas, aar, *aasem, j)
        a2a_wait_recv(aas, aar, *aasem)
        put_rows(abuf, [aar[p].astype(F32) for p in range(ROWS)])

        ds_, dr_ = d_s.at[layer], d_r.at[layer]
        dsem = (rssem.at[layer, 3], rrsem.at[layer, 3])

        def d_body(i, slots):
            y = jnp.zeros((ROWS * RB, CW), F32)
            for k, s in enumerate(slots):
                y = y + jnp.dot(abuf[:, k * KD:(k + 1) * KD], wbuf[s, 0:KD], preferred_element_type=F32)
            rs_send(ds_, dr_, *dsem, i * CW, y)

        run_phase(layer, BASE['d'], 6, 4, True, d_body)
        residual(ds_, dr_, dsem, 1)

    final = [x_r[LAYERS - 1, 1, p].astype(F32) for p in range(ROWS)]
    out0[...] = jnp.concatenate([f[0:4] for f in final], axis=0).astype(BF16)
    out1[...] = jnp.concatenate([f[4:8] for f in final], axis=0).astype(BF16)

    pltpu.make_async_remote_copy(is_recv, is_recv, isem.at[0], isem.at[1], device_id=dev(c, r), device_id_type=MESH).wait_send()

    @pl.when(home)
    def _():
        three = xi_send.at[pl.ds(0, 3)]
        pltpu.make_async_remote_copy(three, three, xisem.at[0], xisem.at[1], device_id=dev(c, r), device_id_type=MESH).wait_send()

    for layer in range(LAYERS):
        for ph, (send, recv) in enumerate(((qkv_s, qkv_r), (o_s, o_r), (gu_s, gu_r), (d_s, d_r))):
            rs_wait_send(send.at[layer], rssem.at[layer, ph], rrsem.at[layer, ph])
        for ph, (send, recv) in enumerate(((ao_s.at[layer], ao_r.at[layer]), (x_s.at[layer, 0], x_r.at[layer, 0]),
                                           (x_s.at[layer, 1], x_r.at[layer, 1]), (aa_s.at[layer], aa_r.at[layer]))):
            a2a_wait_send(send, recv, assem.at[layer, ph], arsem.at[layer, ph])
        for which in range(2):
            if layer == LAYERS - 1 and which == 1:
                continue
            seven = st_r.at[layer, which, pl.ds(0, COLS * ROWS - 1)]
            pltpu.make_async_remote_copy(seven, seven, stsem.at[layer, which, 0], stsem.at[layer, which, 1],
                                         device_id=dev(c, r), device_id_type=MESH).wait_send()
    for copy in out_copies:
        copy.wait()


def solution(mesh):
    hidden_spec = P('rep', 'row')
    index_spec = P(('rep', 'row'))
    cache_spec = P(None, ('rep', 'row'), None, 'col', None)
    gain_spec = P(None, 'row')
    weight_spec = P(None, 'row', 'col')

    def device_program(hidden_0, hidden_1, positions, lengths, cache_k, cache_v, norm_attn, norm_mlp,
                       w_query, w_key, w_value, w_out, w_gate, w_up, w_down):
        cache_shape = cache_k.shape
        flat = (LAYERS, SEQS, CTX * KVH, HD)
        any_spec = pl.BlockSpec(memory_space=pl.ANY)
        smem = pl.BlockSpec(memory_space=pltpu.SMEM)
        vmem = pl.BlockSpec(memory_space=pltpu.VMEM)
        V = pltpu.VMEM
        DMA = pltpu.SemaphoreType.DMA
        scratch = [
            V((NS, D, CW), BF16), V(flat, BF16), V(flat, BF16), V((2, 16, D), BF16),
            V((LAYERS, D), BF16), V((LAYERS, D), BF16), V((ROWS * RB, D), BF16), V((ROWS * RB, FK), BF16), V((RB, QW), F32),
            V((QH * RB, HD), F32), V((KVH * RB, HD), F32), V((KVH * RB, HD), F32), V((QH * RB, HD), F32),
            V((2 * QH, CTX * KVH), jnp.int32), V((RB, HD), F32), V((RB, HD), F32),
            V((ROWS, RB, 128), F32), V((3, ROWS, RB, 128), F32), V((ROWS, RB, D), BF16), V((2, RB, D), BF16),
            V((LAYERS, ROWS, RB, QKV_N), BF16), V((LAYERS, 3, RB, QKV_N), BF16),
            V((LAYERS, ROWS, RB, QW), BF16), V((LAYERS, 3, RB, QW), BF16),
            V((LAYERS, ROWS, RB, 2 * FF), BF16), V((LAYERS, 3, RB, 2 * FF), BF16),
            V((LAYERS, ROWS, RB, QW), BF16), V((LAYERS, 3, RB, QW), BF16),
            V((LAYERS, 2, RB, D), BF16), V((LAYERS, ROWS, RB, D), BF16),
            V((LAYERS, 2, 2, RB, D), BF16), V((LAYERS, 2, ROWS, RB, D), BF16),
            V((LAYERS, 2, RB, FK), BF16), V((LAYERS, ROWS, RB, FK), BF16),
            V((LAYERS, 2, RB, 128), F32), V((LAYERS, 2, COLS * ROWS, RB, 128), F32),
            DMA((NS,)), DMA((6,)), DMA((4,)), DMA((2,)), DMA((3,)),
            DMA((LAYERS, 4)), DMA((LAYERS, 4)), DMA((LAYERS, 4, 4)), DMA((LAYERS, 4, 4)), DMA((LAYERS, 2, 2)),
        ]
        out = pl.pallas_call(
            mega_kernel,
            out_shape=(jax.ShapeDtypeStruct(hidden_0.shape, BF16), jax.ShapeDtypeStruct(hidden_1.shape, BF16),
                       jax.ShapeDtypeStruct(flat, BF16), jax.ShapeDtypeStruct(flat, BF16)),
            in_specs=[any_spec, any_spec, smem, smem] + [any_spec] * 11,
            out_specs=(vmem, vmem, any_spec, any_spec),
            scratch_shapes=scratch,
            compiler_params=pltpu.CompilerParams(collective_id=0, has_side_effects=True, vmem_limit_bytes=67043328),
        )(hidden_0, hidden_1, positions, lengths, cache_k.reshape(flat), cache_v.reshape(flat), norm_attn, norm_mlp,
          w_query, w_key, w_value, w_out, w_gate, w_up, w_down)
        return out[0], out[1], out[2].reshape(cache_shape), out[3].reshape(cache_shape)

    return jax.shard_map(device_program, mesh=mesh,
                         in_specs=(hidden_spec, hidden_spec, index_spec, index_spec, cache_spec, cache_spec, gain_spec, gain_spec) + (weight_spec,) * 7,
                         out_specs=(hidden_spec, hidden_spec, cache_spec, cache_spec), check_vma=False)
```

time: 770 us -> 133 us (0.17); the launches traced: 758 us -> 133 us
  waiting for transfers between devices: 335 us -> 0 us
  matrix products: 183 us -> 0 us
  blocking collectives: 144 us -> 0 us
  Pallas kernels: 0 us -> 124 us
  starting transfers between devices: 36.9 us -> 0 us
  other arithmetic: 25.1 us -> 0 us
  between operations: 16.1 us -> 0.65 us
  local copies, waits for them, and re-layouts: 18.1 us -> 7.95 us
    unnamed x24 -> x0, waiting for transfers between devices: 314 us -> none
    dot_general x36 -> x0, matrix products: 183 us -> none  [the longest x4 42.2 us: decoder_layer(): jnp.dot(to_row_features(activated), w_down[layer], preferred_element_type...]
    pallas_call x0 -> x1, Pallas kernels: none -> 124 us  [device_program(): pl.pallas_call(mega_kernel, out_shape=(jax.ShapeDtypeStruct(hidden_0.shap...]
    all_gather x16 -> x0, blocking collectives: 73.9 us -> none  [to_row_features(): whole = lax.all_gather(block, 'col', axis=1, tiled=True)]
    psum x6 -> x0, blocking collectives: 37.9 us -> none  [rms_norm(): lax.psum(jnp.sum(hidden_f * hidden_f, axis=-1, keepdims=True), 'row')]
    all_to_all x11 -> x0, starting transfers between devices: 36.2 us -> none  [to_row_features(): return lax.all_to_all(whole, 'row', 1, 0, tiled=True)]
    all_to_all x5 -> x0, blocking collectives: 32.5 us -> none  [to_row_features(): return lax.all_to_all(whole, 'row', 1, 0, tiled=True)]
    all_to_all x11 -> x0, waiting for transfers between devices: 20.9 us -> none  [to_row_features(): return lax.all_to_all(whole, 'row', 1, 0, tiled=True)]
  transfers between devices with their start and end apart: 23 -> 0, of which waited for: 18 -> 0; matrix products, arithmetic and copies ran while one was open for 3% -> 0% of each run, Pallas kernels for 0% -> 0%
where the time goes in v1:
time: 133 us
  Pallas kernels  124 us (93%)
  local copies, waits for them, and re-layouts  7.95 us (6%)
    pallas_call x1, Pallas kernels, device_program(): pl.pallas_call(mega_kernel, out_shape=(jax.ShapeDtypeStruct(hidden_0.shap...  124 us
    unnamed x4, local copies, waits for them, and re-layouts  7.95 us

profile of v1, /device:TPU:0, one launch (start us, length us, event | category | flops | bytes accessed | tf_op | source)
XLA Modules:
  0.0 132.5 jit_solution(3897363056268213499)
XLA Ops:
  0.6 123.9 %shard_map.174 = (bf16[16,1536]{1,0:T(8,128)(2,1)}, bf16[16,1536]{1,0:T(8,128)(2,1)}, bf16[2,4,512,128]{3,2,1,0:T(8,128)(2,1)}, bf16[2,4,512,128]{3,2,1,0:T(8,128)(2,1)}) custom-call(bf16[16,1536]{1,0:T(8,128)(2,1)} %h0.1, bf16[16,1536]{1,0:T(8,128)(2,1)} %h1.1, s32[4]{0:T(128)} %positions.1, s32[4]{0:T(128)} %lengths.1, bf16[2,4,512,128]{3,2,1,0:T(8,128)(2,1)} %bitcast.4, ...), custom_call_target="tpu_custom_call" | custom-call | tf_op jit(solution)/shard_map/pallas_call | solution.py:487
  124.6 1.4 %copy.23 = bf16[16,1536]{1,0:T(8,128)(2,1)} copy(bf16[16,1536]{1,0:T(8,128)(2,1)} %get-tuple-element.16) | data formatting | bytes 98304
  126.0 1.4 %copy.24 = bf16[16,1536]{1,0:T(8,128)(2,1)} copy(bf16[16,1536]{1,0:T(8,128)(2,1)} %get-tuple-element.17) | data formatting | bytes 98304
  127.4 2.6 %copy.25 = bf16[2,4,128,4,128]{4,3,2,1,0:T(4,128)(2,1)} copy(bf16[2,4,128,4,128]{4,3,2,1,0:T(4,128)(2,1)} %bitcast.7) | data formatting | bytes 2097152
  130.0 2.6 %copy.26 = bf16[2,4,128,4,128]{4,3,2,1,0:T(4,128)(2,1)} copy(bf16[2,4,128,4,128]{4,3,2,1,0:T(4,128)(2,1)} %bitcast.6) | data formatting | bytes 2097152

commit v2 on v1

--- a/solution.py
+++ b/solution.py
@@ -38,6 +38,12 @@
 PER_LAYER = len(KINDS)
 TOTAL = LAYERS * PER_LAYER
 BASE = {'qkv': 0, 'o': 8, 'gu': 14, 'd': 46}
+NP = 4
+DN = 6
+GT = 8
+GB = 4 * CW
+LAG = 1
+RELAYED = (0, 1, 2)
 
 
 def chunk_of(seq):
@@ -48,13 +54,13 @@
 
 
 def mega_kernel(h0, h1, positions, lengths, ck, cv, na, nm, wq, wk, wv, wo, wg, wu, wd,
-                out0, out1, kout, vout,
-                wbuf, kbuf, vbuf, hbuf, gabuf, gmbuf, nbuf, abuf, xown,
+                out0, out1, kbuf, vbuf,
+                wbuf, hbuf, gabuf, gmbuf, nbuf, abuf, xown,
                 q_scr, kn_scr, vn_scr, o_scr, lim_scr, cos_scr, sin_scr,
                 is_send, is_recv, xi_send, xi_recv,
-                qkv_s, qkv_r, o_s, o_r, gu_s, gu_r, d_s, d_r,
-                ao_s, ao_r, x_s, x_r, aa_s, aa_r, st_s, st_r,
-                wsem, lsem, csem, isem, xisem, rssem, rrsem, assem, arsem, stsem):
+                qkv_s, qkv_r, o_s, o_r, gd_s, gd_r, gk, gx_s, gx_r, d_s, d_r, dacc,
+                ao_s, ao_r, x_s, x_r, aa_s, aa_r, aa_m, st_s, st_r,
+                wsem, lsem, isem, xisem, rssem, rrsem, assem, arsem, stsem, gdsem, gdrem, gxsem, gxrem, acsem, acrem):
     c = lax.axis_index('col')
     r = lax.axis_index('row')
     rep = lax.axis_index('rep')
@@ -75,10 +81,12 @@
 
     def weight_copy(layer, kind, idx, slot):
         if kind == 'd':
-            n, k = idx // 4, idx % 4
+            k, n = idx // DN, idx % DN
             src = wd.at[layer, pl.ds(pl.multiple_of(k * KD, KD), KD), pl.ds(pl.multiple_of(n * CW, CW), CW)]
             return pltpu.make_async_copy(src, wbuf.at[slot, pl.ds(0, KD)], wsem.at[slot])
         ref = {'k': wk, 'v': wv, 'q': wq, 'o': wo, 'g': wg, 'u': wu}[kind]
+        if kind in 'gu':
+            idx = 8 * ((idx % 4) // 2) + 2 * (idx // 4) + idx % 2
         src = ref.at[layer, :, pl.ds(pl.multiple_of(idx * CW, CW), CW)]
         return pltpu.make_async_copy(src, wbuf.at[slot], wsem.at[slot])
 
@@ -92,7 +100,7 @@
         seq = lo
         while seq < hi:
             layer, kind, idx = chunk_of(seq)
-            weight_copy(layer, kind, idx, seq % NS).start()
+            weight_copy(layer, kind, idx, seq % NS).start(priority=1)
             seq += 1
 
     issue_initial(0, 8)
@@ -100,7 +108,7 @@
         copy.start()
     issue_initial(8, NS)
 
-    def run_phase(layer, base, iters, per, down, body):
+    def run_phase(layer, base, lo, iters, per, down, body):
         start = layer * PER_LAYER + base
 
         def future(t):
@@ -109,7 +117,7 @@
         def signature(t):
             return [None if f is None else f[:2] for f in future(t)]
 
-        t = 0
+        t = lo
         while t < iters:
             end = t + 1
             while end < iters and signature(end) == signature(t):
@@ -130,7 +138,7 @@
                 body(i, slots)
                 for f, st, s in zip(first, step, slots):
                     if f is not None:
-                        weight_copy(f[0], f[1], f[2] + st * (i - t), s).start()
+                        weight_copy(f[0], f[1], f[2] + st * (i - t), s).start(priority=1)
                 return carry
 
             if end - t == 1:
@@ -141,7 +149,7 @@
 
     def rs_send(send, recv, ssem, rsem, off, value):
         width = value.shape[1]
-        cols = pl.ds(pl.multiple_of(off, width), width)
+        cols = pl.ds(off if isinstance(off, int) else pl.multiple_of(off, width), width)
         for p in range(ROWS):
             send[p, :, cols] = value[p * RB:(p + 1) * RB].astype(BF16)
         for d in (2, 3, 1):
@@ -194,6 +202,93 @@
                 @pl.when(jnp.logical_not(a2a_self(j, cc)))
                 def _():
                     a2a_copy(send, recv, ssem, rsem, j, cc).wait_send()
+
+    core, chip = lax.rem(r, 2), r // 2
+    sibling = r + 1 - 2 * core
+    across = 2 * (1 - chip) + core
+
+    def act_near(layer, h, j):
+        return pltpu.make_async_remote_copy(aa_s.at[layer, h, j], aa_r.at[layer, h, r], acsem.at[layer, h, j], acrem.at[layer, h, r],
+                                            device_id=dev(c, 2 * c + j), device_id_type=MESH)
+
+    def act_far(layer, h, j):
+        return pltpu.make_async_remote_copy(aa_s.at[layer, h, j], aa_r.at[layer, h, r], acsem.at[layer, h, 2 + j], acrem.at[layer, h, r],
+                                            device_id=dev(1 - c, 2 * c + j), device_id_type=MESH)
+
+    def act_hand(layer, h):
+        return pltpu.make_async_remote_copy(aa_s.at[layer, h], aa_m.at[layer, h], acsem.at[layer, h, 4], acrem.at[layer, h, 4],
+                                            device_id=dev(1 - c, r), device_id_type=MESH)
+
+    def act_forward(layer, h, j):
+        return pltpu.make_async_remote_copy(aa_m.at[layer, h, j], aa_r.at[layer, h, r], acsem.at[layer, h, 5 + j], acrem.at[layer, h, r],
+                                            device_id=dev(c, 2 * (1 - c) + j), device_id_type=MESH)
+
+    def act_diag(layer, h, j):
+        return pltpu.make_async_remote_copy(aa_s.at[layer, h, j], aa_r.at[layer, h, r], acsem.at[layer, h, 2 + j], acrem.at[layer, h, r],
+                                            device_id=dev(1 - c, 2 * c + j), device_id_type=MESH)
+
+    def act_send(layer, h):
+        @pl.when(jnp.logical_not(home))
+        def _():
+            if h in RELAYED:
+                act_hand(layer, h).start()
+            else:
+                for j in range(2):
+                    act_diag(layer, h, j).start()
+            for j in range(2):
+                act_near(layer, h, j).start()
+
+        @pl.when(home)
+        def _():
+            for j in range(2):
+                act_far(layer, h, j).start()
+            for j in range(2):
+                @pl.when(core != j)
+                def _():
+                    act_near(layer, h, j).start()
+
+                @pl.when(core == j)
+                def _():
+                    aa_r[layer, h, r] = aa_s[layer, h, j]
+
+    def act_relay(layer, h):
+        if h not in RELAYED:
+            return
+
+        @pl.when(home)
+        def _():
+            act_hand(layer, h).wait_recv()
+            for j in range(2):
+                act_forward(layer, h, j).start()
+
+    def act_wait(layer, h):
+        for s in range(ROWS):
+            @pl.when(jnp.logical_not(jnp.logical_and(home, r == s)))
+            def _():
+                pltpu.make_async_remote_copy(aa_s.at[layer, h, 0], aa_r.at[layer, h, s], acsem.at[layer, h, 0], acrem.at[layer, h, s],
+                                             device_id=dev(c, r), device_id_type=MESH).wait_recv()
+
+    def act_wait_send(layer, h):
+        @pl.when(jnp.logical_not(home))
+        def _():
+            if h in RELAYED:
+                act_hand(layer, h).wait_send()
+            else:
+                for j in range(2):
+                    act_diag(layer, h, j).wait_send()
+            for j in range(2):
+                act_near(layer, h, j).wait_send()
+
+        @pl.when(home)
+        def _():
+            for j in range(2):
+                act_far(layer, h, j).wait_send()
+                if h in RELAYED:
+                    act_forward(layer, h, j).wait_send()
+
+                @pl.when(core != j)
+                def _():
+                    act_near(layer, h, j).wait_send()
 
     def stat_copy(send, recv, ssem, rsem, e):
         tgt = lax.rem(me + e, COLS * ROWS)
@@ -272,7 +367,6 @@
     for copy in small[4:]:
         copy.wait()
 
-    out_copies = []
     for layer in range(LAYERS):
         qs, qr = qkv_s.at[layer], qkv_r.at[layer]
         qsem = (rssem.at[layer, 0], rrsem.at[layer, 0])
@@ -280,9 +374,9 @@
         def qkv_body(i, slots):
             lhs = nbuf[...]
             y = [jnp.dot(lhs, wbuf[s], preferred_element_type=F32) for s in slots]
-            rs_send(qs, qr, *qsem, i * (2 * CW), jnp.concatenate(y, axis=1))
-
-        run_phase(layer, BASE['qkv'], 4, 2, False, qkv_body)
+            rs_send(qs, qr, *qsem, i * (4 * CW), jnp.concatenate(y, axis=1))
+
+        run_phase(layer, BASE['qkv'], 0, 2, 4, False, qkv_body)
         rs_wait_recv(qr, *qsem)
 
         cosv, sinv = cos_scr[...], sin_scr[...]
@@ -329,10 +423,6 @@
                 hh = j * (QH // 2) + h
                 aos[j, :, h * HD:(h + 1) * HD] = o_scr[hh * RB:(hh + 1) * RB, :].astype(BF16)
             a2a_send(aos, aor, *aosem, j)
-        for which, (buf, out) in enumerate(((kbuf, kout), (vbuf, vout))):
-            copy = pltpu.make_async_copy(buf.at[layer], out.at[layer], csem.at[2 * layer + which])
-            copy.start()
-            out_copies.append(copy)
         a2a_wait_recv(aos, aor, *aosem)
         put_rows(nbuf, [aor[p].astype(F32) for p in range(ROWS)])
 
@@ -350,7 +440,7 @@
         def o_body(i, slots):
             lhs = nbuf[...]
             y = [jnp.dot(lhs, wbuf[s], preferred_element_type=F32) for s in slots]
-            rs_send(os_, or_, *osem, i * (2 * CW), jnp.concatenate(y, axis=1))
+            rs_send(os_, or_, *osem, i * (3 * CW), jnp.concatenate(y, axis=1))
 
         def residual(send, recv, sems, which):
             rs_wait_recv(recv, *sems)
@@ -387,41 +477,88 @@
                 parts.append(normalise(p, xr[p].astype(F32), stv[p] + stv[ROWS + p], g))
             put_rows(nbuf, parts)
 
-        run_phase(layer, BASE['o'], 3, 2, False, o_body)
+        run_phase(layer, BASE['o'], 0, 2, 3, False, o_body)
         residual(os_, or_, osem, 0)
 
-        gs, gr = gu_s.at[layer], gu_r.at[layer]
-        gsem = (rssem.at[layer, 2], rrsem.at[layer, 2])
+        def gu_cols(i):
+            return pl.ds(i * GB if isinstance(i, int) else pl.multiple_of(i * GB, GB), GB)
 
         def gu_body(i, slots):
             lhs = nbuf[...]
-            y = [jnp.dot(lhs, wbuf[s], preferred_element_type=F32) for s in slots]
-            rs_send(gs, gr, *gsem, i * (2 * CW), jnp.concatenate(y, axis=1))
-
-        run_phase(layer, BASE['gu'], 16, 2, False, gu_body)
-        rs_wait_recv(gr, *gsem)
-        aas, aar = aa_s.at[layer], aa_r.at[layer]
-        aasem = (assem.at[layer, 3], arsem.at[layer, 3])
-        for j in range(2):
-            for i in range(8):
-                lo = (j * 8 + i) * 2 * CW
-                gate = rs_sum(gs, gr, lo, lo + CW).astype(BF16).astype(F32)
-                up = rs_sum(gs, gr, lo + CW, lo + 2 * CW).astype(BF16).astype(F32)
-                aas[j, :, i * CW:(i + 1) * CW] = (gate * jax.nn.sigmoid(gate) * up).astype(BF16)
-            a2a_send(aas, aar, *aasem, j)
-        a2a_wait_recv(aas, aar, *aasem)
-        put_rows(abuf, [aar[p].astype(F32) for p in range(ROWS)])
+            y = jnp.concatenate([jnp.dot(lhs, wbuf[s], preferred_element_type=F32) for s in slots], axis=1)
+            cols = gu_cols(i)
+            for p in range(2):
+                even, odd = y[2 * p * RB:(2 * p + 1) * RB], y[(2 * p + 1) * RB:(2 * p + 2) * RB]
+                gk[p, :, cols] = jnp.where(core == 0, even, odd)
+                gd_s[layer, p, :, cols] = jnp.where(core == 0, odd, even).astype(BF16)
+            pltpu.make_async_remote_copy(gd_s.at[layer, :, :, cols], gd_r.at[layer, :, :, cols], gdsem.at[layer], gdrem.at[layer, i],
+                                         device_id=dev(c, sibling), device_id_type=MESH).start()
+
+            @pl.when(i >= LAG)
+            def _():
+                pair_sum(i - LAG)
+
+        def pair_sum(i):
+            cols = gu_cols(i)
+            pltpu.make_async_remote_copy(gd_s.at[layer, :, :, cols], gd_r.at[layer, :, :, cols], gdsem.at[layer], gdrem.at[layer, i],
+                                         device_id=dev(c, sibling), device_id_type=MESH).wait_recv()
+            s0 = gk[0, :, cols] + gd_r[layer, 0, :, cols].astype(F32)
+            s1 = gk[1, :, cols] + gd_r[layer, 1, :, cols].astype(F32)
+            gk[0, :, cols] = jnp.where(chip == 0, s0, s1)
+            gx_s[layer, :, cols] = jnp.where(chip == 0, s1, s0).astype(BF16)
+            pltpu.make_async_remote_copy(gx_s.at[layer, :, cols], gx_r.at[layer, :, cols], gxsem.at[layer], gxrem.at[layer, i // (GT // NP)],
+                                         device_id=dev(c, across), device_id_type=MESH).start()
+
+        def activate(q):
+            width = GT // NP * GB
+            ref = gx_r.at[layer, :, pl.ds(q * width, width)]
+            pltpu.make_async_remote_copy(ref, ref, gxsem.at[layer], gxrem.at[layer, q], device_id=dev(c, r), device_id_type=MESH).wait_recv()
+            for j in range(2):
+                for w in range(2):
+                    lo = q * width + (2 * j + w) * 2 * CW
+                    mid, hi = lo + CW, lo + 2 * CW
+                    gate = (gk[0, :, lo:mid] + gx_r[layer, :, lo:mid].astype(F32)).astype(BF16).astype(F32)
+                    up = (gk[0, :, mid:hi] + gx_r[layer, :, mid:hi].astype(F32)).astype(BF16).astype(F32)
+                    aa_s[layer, q, j, :, w * CW:(w + 1) * CW] = (gate * jax.nn.sigmoid(gate) * up).astype(BF16)
+            act_send(layer, q)
 
         ds_, dr_ = d_s.at[layer], d_r.at[layer]
-        dsem = (rssem.at[layer, 3], rrsem.at[layer, 3])
-
-        def d_body(i, slots):
-            y = jnp.zeros((ROWS * RB, CW), F32)
-            for k, s in enumerate(slots):
-                y = y + jnp.dot(abuf[:, k * KD:(k + 1) * KD], wbuf[s, 0:KD], preferred_element_type=F32)
-            rs_send(ds_, dr_, *dsem, i * CW, y)
-
-        run_phase(layer, BASE['d'], 6, 4, True, d_body)
+        dsem = (rssem.at[layer, 2], rrsem.at[layer, 2])
+
+        def d_part(q):
+            def body(i, slots):
+                lhs = abuf[:, q * KD:(q + 1) * KD]
+                y = [jnp.dot(lhs, wbuf[s, 0:KD], preferred_element_type=F32) for s in slots]
+                y = jnp.concatenate(y, axis=1)
+                cols = slice(i * 3 * CW, (i + 1) * 3 * CW)
+                if q > 0:
+                    y = y + dacc[:, cols]
+                if q < NP - 1:
+                    dacc[:, cols] = y
+                else:
+                    rs_send(ds_, dr_, *dsem, i * (3 * CW), y)
+
+            act_wait(layer, q)
+            abuf[:, q * KD:(q + 1) * KD] = jnp.concatenate([aa_r[layer, q, p].astype(F32) for p in range(ROWS)], axis=0).astype(BF16)
+            for i in range(2):
+                run_phase(layer, BASE['d'] + q * DN, i, i + 1, 3, True, body)
+
+        run_phase(layer, BASE['gu'], 0, 6, 4, False, gu_body)
+        activate(0)
+        run_phase(layer, BASE['gu'], 6, GT, 4, False, gu_body)
+        activate(1)
+        act_relay(layer, 0)
+        for i in range(GT - LAG, GT):
+            pair_sum(i)
+        activate(2)
+        act_relay(layer, 1)
+        d_part(0)
+        activate(3)
+        act_relay(layer, 2)
+        d_part(1)
+        act_relay(layer, 3)
+        d_part(2)
+        d_part(3)
         residual(ds_, dr_, dsem, 1)
 
     final = [x_r[LAYERS - 1, 1, p].astype(F32) for p in range(ROWS)]
@@ -436,19 +573,21 @@
         pltpu.make_async_remote_copy(three, three, xisem.at[0], xisem.at[1], device_id=dev(c, r), device_id_type=MESH).wait_send()
 
     for layer in range(LAYERS):
-        for ph, (send, recv) in enumerate(((qkv_s, qkv_r), (o_s, o_r), (gu_s, gu_r), (d_s, d_r))):
+        for ph, (send, recv) in enumerate(((qkv_s, qkv_r), (o_s, o_r), (d_s, d_r))):
             rs_wait_send(send.at[layer], rssem.at[layer, ph], rrsem.at[layer, ph])
         for ph, (send, recv) in enumerate(((ao_s.at[layer], ao_r.at[layer]), (x_s.at[layer, 0], x_r.at[layer, 0]),
-                                           (x_s.at[layer, 1], x_r.at[layer, 1]), (aa_s.at[layer], aa_r.at[layer]))):
+                                           (x_s.at[layer, 1], x_r.at[layer, 1]))):
             a2a_wait_send(send, recv, assem.at[layer, ph], arsem.at[layer, ph])
+        pltpu.make_async_remote_copy(gd_s.at[layer], gd_s.at[layer], gdsem.at[layer], gdrem.at[layer, 0], device_id=dev(c, r), device_id_type=MESH).wait_send()
+        pltpu.make_async_remote_copy(gx_s.at[layer], gx_s.at[layer], gxsem.at[layer], gxrem.at[layer, 0], device_id=dev(c, r), device_id_type=MESH).wait_send()
+        for h in range(NP):
+            act_wait_send(layer, h)
         for which in range(2):
             if layer == LAYERS - 1 and which == 1:
                 continue
             seven = st_r.at[layer, which, pl.ds(0, COLS * ROWS - 1)]
             pltpu.make_async_remote_copy(seven, seven, stsem.at[layer, which, 0], stsem.at[layer, which, 1],
                                          device_id=dev(c, r), device_id_type=MESH).wait_send()
-    for copy in out_copies:
-        copy.wait()
 
 
 def solution(mesh):
@@ -468,30 +607,33 @@
         V = pltpu.VMEM
         DMA = pltpu.SemaphoreType.DMA
         scratch = [
-            V((NS, D, CW), BF16), V(flat, BF16), V(flat, BF16), V((2, 16, D), BF16),
+            V((NS, D, CW), BF16), V((2, 16, D), BF16),
             V((LAYERS, D), BF16), V((LAYERS, D), BF16), V((ROWS * RB, D), BF16), V((ROWS * RB, FK), BF16), V((RB, QW), F32),
             V((QH * RB, HD), F32), V((KVH * RB, HD), F32), V((KVH * RB, HD), F32), V((QH * RB, HD), F32),
             V((2 * QH, CTX * KVH), jnp.int32), V((RB, HD), F32), V((RB, HD), F32),
             V((ROWS, RB, 128), F32), V((3, ROWS, RB, 128), F32), V((ROWS, RB, D), BF16), V((2, RB, D), BF16),
             V((LAYERS, ROWS, RB, QKV_N), BF16), V((LAYERS, 3, RB, QKV_N), BF16),
             V((LAYERS, ROWS, RB, QW), BF16), V((LAYERS, 3, RB, QW), BF16),
-            V((LAYERS, ROWS, RB, 2 * FF), BF16), V((LAYERS, 3, RB, 2 * FF), BF16),
-            V((LAYERS, ROWS, RB, QW), BF16), V((LAYERS, 3, RB, QW), BF16),
+            V((LAYERS, 2, RB, 2 * FF), BF16), V((LAYERS, 2, RB, 2 * FF), BF16), V((2, RB, 2 * FF), F32),
+            V((LAYERS, RB, 2 * FF), BF16), V((LAYERS, RB, 2 * FF), BF16),
+            V((LAYERS, ROWS, RB, QW), BF16), V((LAYERS, 3, RB, QW), BF16), V((ROWS * RB, QW), F32),
             V((LAYERS, 2, RB, D), BF16), V((LAYERS, ROWS, RB, D), BF16),
             V((LAYERS, 2, 2, RB, D), BF16), V((LAYERS, 2, ROWS, RB, D), BF16),
-            V((LAYERS, 2, RB, FK), BF16), V((LAYERS, ROWS, RB, FK), BF16),
+            V((LAYERS, NP, 2, RB, KD), BF16), V((LAYERS, NP, ROWS, RB, KD), BF16), V((LAYERS, NP, 2, RB, KD), BF16),
             V((LAYERS, 2, RB, 128), F32), V((LAYERS, 2, COLS * ROWS, RB, 128), F32),
-            DMA((NS,)), DMA((6,)), DMA((4,)), DMA((2,)), DMA((3,)),
-            DMA((LAYERS, 4)), DMA((LAYERS, 4)), DMA((LAYERS, 4, 4)), DMA((LAYERS, 4, 4)), DMA((LAYERS, 2, 2)),
+            DMA((NS,)), DMA((6,)), DMA((2,)), DMA((3,)),
+            DMA((LAYERS, 3)), DMA((LAYERS, 3)), DMA((LAYERS, 3, 4)), DMA((LAYERS, 3, 4)), DMA((LAYERS, 2, 2)),
+            DMA((LAYERS,)), DMA((LAYERS, GT)), DMA((LAYERS,)), DMA((LAYERS, NP)), DMA((LAYERS, NP, 7)), DMA((LAYERS, NP, 5)),
         ]
+        shapes = (hidden_0.shape, hidden_1.shape, flat, flat)
+        results = tuple(V(shape, BF16) for shape in shapes)
         out = pl.pallas_call(
             mega_kernel,
-            out_shape=(jax.ShapeDtypeStruct(hidden_0.shape, BF16), jax.ShapeDtypeStruct(hidden_1.shape, BF16),
-                       jax.ShapeDtypeStruct(flat, BF16), jax.ShapeDtypeStruct(flat, BF16)),
+            out_shape=results,
             in_specs=[any_spec, any_spec, smem, smem] + [any_spec] * 11,
-            out_specs=(vmem, vmem, any_spec, any_spec),
+            out_specs=(vmem,) * 4,
             scratch_shapes=scratch,
-            compiler_params=pltpu.CompilerParams(collective_id=0, has_side_effects=True, vmem_limit_bytes=67043328),
+            compiler_params=pltpu.CompilerParams(collective_id=0, has_side_effects=True, vmem_limit_bytes=63000000),
         )(hidden_0, hidden_1, positions, lengths, cache_k.reshape(flat), cache_v.reshape(flat), norm_attn, norm_mlp,
           w_query, w_key, w_value, w_out, w_gate, w_up, w_down)
         return out[0], out[1], out[2].reshape(cache_shape), out[3].reshape(cache_shape)

time: 133 us -> 107 us (0.80)
  Pallas kernels: 124 us -> 103 us
  local copies, waits for them, and re-layouts: 7.95 us -> 3.18 us
    pallas_call x1, Pallas kernels: 124 us -> 103 us  [device_program(): pl.pallas_call(mega_kernel, out_shape=results, in_specs=[any_spec, any_sp...]
    unnamed x4, local copies, waits for them, and re-layouts: 7.95 us -> 3.18 us
where the time goes in v2:
time: 107 us
  Pallas kernels  103 us (96%)
  local copies, waits for them, and re-layouts  3.18 us (3%)
    pallas_call x1, Pallas kernels, device_program(): pl.pallas_call(mega_kernel, out_shape=results, in_specs=[any_spec, any_sp...  103 us
    unnamed x4, local copies, waits for them, and re-layouts  3.18 us

profile of v2, /device:TPU:0, one launch (start us, length us, event | category | flops | bytes accessed | tf_op | source)
XLA Modules:
  0.0 107.1 jit_solution(9181458664278893350)
XLA Ops:
  0.6 103.3 %shard_map.174 = (bf16[16,1536]{1,0:T(8,128)(2,1)S(1)}, bf16[16,1536]{1,0:T(8,128)(2,1)S(1)}, bf16[2,4,512,128]{3,2,1,0:T(8,128)(2,1)S(1)}, bf16[2,4,512,128]{3,2,1,0:T(8,128)(2,1)S(1)}) custom-call(bf16[16,1536]{1,0:T(8,128)(2,1)} %h0.1, bf16[16,1536]{1,0:T(8,128)(2,1)} %h1.1, s32[4]{0:T(128)} %positions.1, s32[4]{0:T(128)} %lengths.1, ...), custom_call_target="tpu_custom_call" | custom-call | tf_op jit(solution)/shard_map/pallas_call | solution.py:630
  103.9 0.6 copy.23
  104.5 0.6 copy.24
  105.2 1.0 copy.25
  106.1 1.0 copy.26

commit v3 on v2

--- a/solution.py
+++ b/solution.py
@@ -43,7 +43,7 @@
 GT = 8
 GB = 4 * CW
 LAG = 1
-RELAYED = (0, 1, 2)
+RELAYED = (1,)
 
 
 def chunk_of(seq):
@@ -371,13 +371,23 @@
         qs, qr = qkv_s.at[layer], qkv_r.at[layer]
         qsem = (rssem.at[layer, 0], rrsem.at[layer, 0])
 
-        def qkv_body(i, slots):
+        def lhs_dots(slots):
             lhs = nbuf[...]
-            y = [jnp.dot(lhs, wbuf[s], preferred_element_type=F32) for s in slots]
-            rs_send(qs, qr, *qsem, i * (4 * CW), jnp.concatenate(y, axis=1))
-
-        run_phase(layer, BASE['qkv'], 0, 2, 4, False, qkv_body)
-        rs_wait_recv(qr, *qsem)
+            return jnp.concatenate([jnp.dot(lhs, wbuf[s], preferred_element_type=F32) for s in slots], axis=1)
+
+        early = 4 * CW
+
+        def qkv_first(i, slots):
+            rs_send(qs, qr, qsem[0], rrsem.at[layer, 3], 0, lhs_dots(slots))
+
+        def qkv_rest(i, slots):
+            off = i * (2 * CW) + early
+            rs_send(qs, qr, *qsem, off, lhs_dots(slots))
+
+        run_phase(layer, BASE['qkv'], 0, 1, 4, False, qkv_first)
+        run_phase(layer, BASE['qkv'] + 4, 0, 2, 2, False, qkv_rest)
+        part = qr.at[:, :, pl.ds(0, early)]
+        pltpu.make_async_remote_copy(part, part, qsem[0], rrsem.at[layer, 3], device_id=dev(c, r), device_id_type=MESH).wait_recv()
 
         cosv, sinv = cos_scr[...], sin_scr[...]
 
@@ -388,8 +398,11 @@
         for h in range(KVH):
             kn_scr[h * RB:(h + 1) * RB, :] = rope(rs_sum(qs, qr, h * HD, (h + 1) * HD))
             vn_scr[h * RB:(h + 1) * RB, :] = rs_sum(qs, qr, KVW + h * HD, KVW + (h + 1) * HD)
-        for h in range(QH):
-            q_scr[h * RB:(h + 1) * RB, :] = rope(rs_sum(qs, qr, 2 * KVW + h * HD, 2 * KVW + (h + 1) * HD))
+        def query(lo, hi):
+            for h in range(lo, hi):
+                q_scr[h * RB:(h + 1) * RB, :] = rope(rs_sum(qs, qr, 2 * KVW + h * HD, 2 * KVW + (h + 1) * HD))
+
+        query(0, 8)
         row_slot = jnp.right_shift(lax.broadcasted_iota(jnp.int32, (CTX * KVH, HD), 0), 2)
         for b in range(SEQS):
             length = lengths[b]
@@ -403,19 +416,25 @@
                     value = jnp.where(row_slot == length + s, full, value)
                 return value.astype(BF16)
 
-            keys = updated(kbuf, kn_scr)
-            vals = updated(vbuf, vn_scr)
-            kbuf[layer, b] = keys
-            vbuf[layer, b] = vals
+            kbuf[layer, b] = updated(kbuf, kn_scr)
+            vbuf[layer, b] = updated(vbuf, vn_scr)
+
+        part = qr.at[:, :, pl.ds(early, QKV_N - early)]
+        pltpu.make_async_remote_copy(part, part, *qsem, device_id=dev(c, r), device_id_type=MESH).wait_recv()
+        query(8, QH)
+        scores = []
+        for b in range(SEQS):
             qb = jnp.concatenate([q_scr[pl.ds(b + SEQS * s, QH, stride=RB), :] for s in range(2)], axis=0).astype(BF16)
-            scores = lax.dot_general(qb, keys, (((1,), (1,)), ((), ())), preferred_element_type=F32) * (HD ** -0.5)
-            scores = jnp.where(lim_scr[...] <= length, scores, -jnp.inf)
-            top = jnp.max(scores, axis=1, keepdims=True)
-            e = jnp.exp(scores - top)
-            probs = (e / jnp.sum(e, axis=1, keepdims=True)).astype(BF16)
-            ob = jnp.dot(probs, vals, preferred_element_type=F32)
+            scores.append(lax.dot_general(qb, kbuf[layer, b], (((1,), (1,)), ((), ())), preferred_element_type=F32))
+        probs = []
+        for b in range(SEQS):
+            sc = jnp.where(lim_scr[...] <= lengths[b], scores[b] * (HD ** -0.5), -jnp.inf)
+            e = jnp.exp(sc - jnp.max(sc, axis=1, keepdims=True))
+            probs.append((e / jnp.sum(e, axis=1, keepdims=True)).astype(BF16))
+        outs = [jnp.dot(probs[b], vbuf[layer, b], preferred_element_type=F32) for b in range(SEQS)]
+        for b in range(SEQS):
             for s in range(2):
-                o_scr[pl.ds(b + SEQS * s, QH, stride=RB), :] = ob[s * QH:(s + 1) * QH]
+                o_scr[pl.ds(b + SEQS * s, QH, stride=RB), :] = outs[b][s * QH:(s + 1) * QH]
         aos, aor = ao_s.at[layer], ao_r.at[layer]
         aosem = (assem.at[layer, 0], arsem.at[layer, 0])
         for j in range(2):
@@ -440,7 +459,7 @@
         def o_body(i, slots):
             lhs = nbuf[...]
             y = [jnp.dot(lhs, wbuf[s], preferred_element_type=F32) for s in slots]
-            rs_send(os_, or_, *osem, i * (3 * CW), jnp.concatenate(y, axis=1))
+            rs_send(os_, or_, *osem, i * (2 * CW), jnp.concatenate(y, axis=1))
 
         def residual(send, recv, sems, which):
             rs_wait_recv(recv, *sems)
@@ -477,7 +496,7 @@
                 parts.append(normalise(p, xr[p].astype(F32), stv[p] + stv[ROWS + p], g))
             put_rows(nbuf, parts)
 
-        run_phase(layer, BASE['o'], 0, 2, 3, False, o_body)
+        run_phase(layer, BASE['o'], 0, 3, 2, False, o_body)
         residual(os_, or_, osem, 0)
 
         def gu_cols(i):
@@ -526,22 +545,24 @@
         dsem = (rssem.at[layer, 2], rrsem.at[layer, 2])
 
         def d_part(q):
-            def body(i, slots):
-                lhs = abuf[:, q * KD:(q + 1) * KD]
-                y = [jnp.dot(lhs, wbuf[s, 0:KD], preferred_element_type=F32) for s in slots]
-                y = jnp.concatenate(y, axis=1)
-                cols = slice(i * 3 * CW, (i + 1) * 3 * CW)
-                if q > 0:
-                    y = y + dacc[:, cols]
-                if q < NP - 1:
-                    dacc[:, cols] = y
-                else:
-                    rs_send(ds_, dr_, *dsem, i * (3 * CW), y)
+            def body(first):
+                def run(i, slots):
+                    lhs = abuf[:, q * KD:(q + 1) * KD]
+                    y = jnp.concatenate([jnp.dot(lhs, wbuf[s, 0:KD], preferred_element_type=F32) for s in slots], axis=1)
+                    lo, hi = first * CW, (first + len(slots)) * CW
+                    if q > 0:
+                        y = y + dacc[:, lo:hi]
+                    if q < NP - 1:
+                        dacc[:, lo:hi] = y
+                        return
+                    for part in range(lo, hi, 2 * CW):
+                        rs_send(ds_, dr_, *dsem, part, y[:, part - lo:part - lo + 2 * CW])
+                return run
 
             act_wait(layer, q)
             abuf[:, q * KD:(q + 1) * KD] = jnp.concatenate([aa_r[layer, q, p].astype(F32) for p in range(ROWS)], axis=0).astype(BF16)
-            for i in range(2):
-                run_phase(layer, BASE['d'] + q * DN, i, i + 1, 3, True, body)
+            for first, count in (((0, DN),) if q < NP - 1 else ((0, 4), (4, 2))):
+                run_phase(layer, BASE['d'] + q * DN + first, 0, 1, count, True, body(first))
 
         run_phase(layer, BASE['gu'], 0, 6, 4, False, gu_body)
         activate(0)
@@ -622,7 +643,7 @@
             V((LAYERS, NP, 2, RB, KD), BF16), V((LAYERS, NP, ROWS, RB, KD), BF16), V((LAYERS, NP, 2, RB, KD), BF16),
             V((LAYERS, 2, RB, 128), F32), V((LAYERS, 2, COLS * ROWS, RB, 128), F32),
             DMA((NS,)), DMA((6,)), DMA((2,)), DMA((3,)),
-            DMA((LAYERS, 3)), DMA((LAYERS, 3)), DMA((LAYERS, 3, 4)), DMA((LAYERS, 3, 4)), DMA((LAYERS, 2, 2)),
+            DMA((LAYERS, 3)), DMA((LAYERS, 4)), DMA((LAYERS, 3, 4)), DMA((LAYERS, 3, 4)), DMA((LAYERS, 2, 2)),
             DMA((LAYERS,)), DMA((LAYERS, GT)), DMA((LAYERS,)), DMA((LAYERS, NP)), DMA((LAYERS, NP, 7)), DMA((LAYERS, NP, 5)),
         ]
         shapes = (hidden_0.shape, hidden_1.shape, flat, flat)

time: 107 us -> 104 us (0.972)
  Pallas kernels: 103 us -> 100 us
    pallas_call x1, Pallas kernels: 103 us -> 100 us  [device_program(): pl.pallas_call(mega_kernel, out_shape=results, in_specs=[any_spec, any_sp...]
where the time goes in v3:
time: 104 us
  Pallas kernels  100 us (96%)
  local copies, waits for them, and re-layouts  3.18 us (3%)
    pallas_call x1, Pallas kernels, device_program(): pl.pallas_call(mega_kernel, out_shape=results, in_specs=[any_spec, any_sp...  100 us
    unnamed x4, local copies, waits for them, and re-layouts  3.18 us

profile of v3, /device:TPU:0, one launch (start us, length us, event | category | flops | bytes accessed | tf_op | source)
XLA Modules:
  0.0 104.1 jit_solution(514194332427103180)
XLA Ops:
  0.6 100.3 %shard_map.174 = (bf16[16,1536]{1,0:T(8,128)(2,1)S(1)}, bf16[16,1536]{1,0:T(8,128)(2,1)S(1)}, bf16[2,4,512,128]{3,2,1,0:T(8,128)(2,1)S(1)}, bf16[2,4,512,128]{3,2,1,0:T(8,128)(2,1)S(1)}) custom-call(bf16[16,1536]{1,0:T(8,128)(2,1)} %h0.1, bf16[16,1536]{1,0:T(8,128)(2,1)} %h1.1, s32[4]{0:T(128)} %positions.1, s32[4]{0:T(128)} %lengths.1, ...), custom_call_target="tpu_custom_call" | custom-call | tf_op jit(solution)/shard_map/pallas_call | solution.py:651
  101.0 0.6 copy.23
  101.6 0.6 copy.24
  102.2 1.0 copy.25
  103.2 1.0 copy.26

commit v4 on v3

--- a/solution.py
+++ b/solution.py
@@ -28,20 +28,20 @@
 FK = 4096
 WIDTH = 6144
 CTX = 128
-CW = 512
+CW = 1024
 KD = 1024
-NS = 30
+NS = 15
 
 QKV_N = QW + 2 * KVW
-KINDS = ['k', 'v'] + ['q'] * 6 + ['o'] * 6 + ['g', 'u'] * 16 + ['d'] * 24
-INDEX = [0, 0] + list(range(6)) + list(range(6)) + [i // 2 for i in range(32)] + list(range(24))
+KINDS = ['kv'] + ['q'] * 3 + ['o'] * 3 + ['g', 'u'] * 8 + ['d'] * 12
+INDEX = [0] + list(range(3)) + list(range(3)) + [i // 2 for i in range(16)] + list(range(12))
 PER_LAYER = len(KINDS)
 TOTAL = LAYERS * PER_LAYER
-BASE = {'qkv': 0, 'o': 8, 'gu': 14, 'd': 46}
+BASE = {'qkv': 0, 'o': 4, 'gu': 7, 'd': 23}
 NP = 4
-DN = 6
+DN = 3
 GT = 8
-GB = 4 * CW
+GB = 2 * CW
 LAG = 1
 RELAYED = (1,)
 
@@ -83,12 +83,15 @@
         if kind == 'd':
             k, n = idx // DN, idx % DN
             src = wd.at[layer, pl.ds(pl.multiple_of(k * KD, KD), KD), pl.ds(pl.multiple_of(n * CW, CW), CW)]
-            return pltpu.make_async_copy(src, wbuf.at[slot, pl.ds(0, KD)], wsem.at[slot])
-        ref = {'k': wk, 'v': wv, 'q': wq, 'o': wo, 'g': wg, 'u': wu}[kind]
-        if kind in 'gu':
-            idx = 8 * ((idx % 4) // 2) + 2 * (idx // 4) + idx % 2
+            return [pltpu.make_async_copy(src, wbuf.at[slot, pl.ds(0, KD)], wsem.at[slot])]
+        if kind == 'kv':
+            return [pltpu.make_async_copy(ref.at[layer], wbuf.at[slot, :, pl.ds(i * KVW, KVW)], wsem.at[slot])
+                    for i, ref in enumerate((wk, wv))]
+        ref = {'q': wq, 'o': wo, 'g': wg, 'u': wu}[kind]
+        if kind in ('g', 'u'):
+            idx = 4 * (idx % 2) + idx // 2
         src = ref.at[layer, :, pl.ds(pl.multiple_of(idx * CW, CW), CW)]
-        return pltpu.make_async_copy(src, wbuf.at[slot], wsem.at[slot])
+        return [pltpu.make_async_copy(src, wbuf.at[slot], wsem.at[slot])]
 
     def weight_wait(down, slot):
         if down:
@@ -100,13 +103,14 @@
         seq = lo
         while seq < hi:
             layer, kind, idx = chunk_of(seq)
-            weight_copy(layer, kind, idx, seq % NS).start(priority=1)
+            for copy in weight_copy(layer, kind, idx, seq % NS):
+                copy.start(priority=1)
             seq += 1
 
-    issue_initial(0, 8)
+    issue_initial(0, 4)
     for copy in small[4:]:
         copy.start()
-    issue_initial(8, NS)
+    issue_initial(4, NS)
 
     def run_phase(layer, base, lo, iters, per, down, body):
         start = layer * PER_LAYER + base
@@ -138,7 +142,8 @@
                 body(i, slots)
                 for f, st, s in zip(first, step, slots):
                     if f is not None:
-                        weight_copy(f[0], f[1], f[2] + st * (i - t), s).start(priority=1)
+                        for copy in weight_copy(f[0], f[1], f[2] + st * (i - t), s):
+                            copy.start(priority=1)
                 return carry
 
             if end - t == 1:
@@ -306,9 +311,11 @@
     h0v = hbuf[0].astype(F32)
     h1v = hbuf[1].astype(F32)
     blocks = [jnp.concatenate([h0v[4 * p:4 * p + 4], h1v[4 * p:4 * p + 4]], axis=0) for p in range(ROWS)]
+    lane_block = jnp.right_shift(lax.broadcasted_iota(jnp.int32, (RB, 128), 1), 5)
+    packed = jnp.zeros((RB, 128), F32)
     for p in range(ROWS):
-        sq = jnp.sum(blocks[p] * blocks[p], axis=1, keepdims=True)
-        is_send[p] = jnp.broadcast_to(sq, (RB, 128))
+        packed = jnp.where(lane_block == p, jnp.sum(blocks[p] * blocks[p], axis=1, keepdims=True), packed)
+    is_send[...] = packed
     for d in (2, 3, 1):
         tgt = lax.rem(r + d, ROWS)
         pltpu.make_async_remote_copy(is_send, is_recv.at[d - 1], isem.at[0], isem.at[1],
@@ -359,9 +366,9 @@
 
     gain = gabuf[0:1, :].astype(F32)
     parts = []
+    packed = is_send[...] + is_recv[0] + is_recv[1] + is_recv[2]
     for p in range(ROWS):
-        total = is_send[p] + is_recv[0, p] + is_recv[1, p] + is_recv[2, p]
-        parts.append(normalise(p, blocks[p], total, gain))
+        parts.append(normalise(p, blocks[p], packed[:, 32 * p:32 * p + 1], gain))
     put_rows(nbuf, parts)
 
     for copy in small[4:]:
@@ -375,17 +382,17 @@
             lhs = nbuf[...]
             return jnp.concatenate([jnp.dot(lhs, wbuf[s], preferred_element_type=F32) for s in slots], axis=1)
 
-        early = 4 * CW
+        early = CW
 
         def qkv_first(i, slots):
             rs_send(qs, qr, qsem[0], rrsem.at[layer, 3], 0, lhs_dots(slots))
 
         def qkv_rest(i, slots):
-            off = i * (2 * CW) + early
+            off = i * CW + early
             rs_send(qs, qr, *qsem, off, lhs_dots(slots))
 
-        run_phase(layer, BASE['qkv'], 0, 1, 4, False, qkv_first)
-        run_phase(layer, BASE['qkv'] + 4, 0, 2, 2, False, qkv_rest)
+        run_phase(layer, BASE['qkv'], 0, 1, 1, False, qkv_first)
+        run_phase(layer, BASE['qkv'] + 1, 0, 3, 1, False, qkv_rest)
         part = qr.at[:, :, pl.ds(0, early)]
         pltpu.make_async_remote_copy(part, part, qsem[0], rrsem.at[layer, 3], device_id=dev(c, r), device_id_type=MESH).wait_recv()
 
@@ -402,7 +409,7 @@
             for h in range(lo, hi):
                 q_scr[h * RB:(h + 1) * RB, :] = rope(rs_sum(qs, qr, 2 * KVW + h * HD, 2 * KVW + (h + 1) * HD))
 
-        query(0, 8)
+        query(0, 0)
         row_slot = jnp.right_shift(lax.broadcasted_iota(jnp.int32, (CTX * KVH, HD), 0), 2)
         for b in range(SEQS):
             length = lengths[b]
@@ -421,7 +428,7 @@
 
         part = qr.at[:, :, pl.ds(early, QKV_N - early)]
         pltpu.make_async_remote_copy(part, part, *qsem, device_id=dev(c, r), device_id_type=MESH).wait_recv()
-        query(8, QH)
+        query(0, QH)
         scores = []
         for b in range(SEQS):
             qb = jnp.concatenate([q_scr[pl.ds(b + SEQS * s, QH, stride=RB), :] for s in range(2)], axis=0).astype(BF16)
@@ -459,7 +466,7 @@
         def o_body(i, slots):
             lhs = nbuf[...]
             y = [jnp.dot(lhs, wbuf[s], preferred_element_type=F32) for s in slots]
-            rs_send(os_, or_, *osem, i * (2 * CW), jnp.concatenate(y, axis=1))
+            rs_send(os_, or_, *osem, i * CW, jnp.concatenate(y, axis=1))
 
         def residual(send, recv, sems, which):
             rs_wait_recv(recv, *sems)
@@ -492,11 +499,11 @@
                                          device_id=dev(c, r), device_id_type=MESH).wait_recv()
             g = (gmbuf[layer:layer + 1, :] if which == 0 else gabuf[layer + 1:layer + 2, :]).astype(F32)
             parts = []
-            for p in range(ROWS):
+            for p in ((r, across, sibling, 2 * (1 - chip) + 1 - core) if which == 0 else range(ROWS)):
                 parts.append(normalise(p, xr[p].astype(F32), stv[p] + stv[ROWS + p], g))
             put_rows(nbuf, parts)
 
-        run_phase(layer, BASE['o'], 0, 3, 2, False, o_body)
+        run_phase(layer, BASE['o'], 0, 3, 1, False, o_body)
         residual(os_, or_, osem, 0)
 
         def gu_cols(i):
@@ -507,9 +514,8 @@
             y = jnp.concatenate([jnp.dot(lhs, wbuf[s], preferred_element_type=F32) for s in slots], axis=1)
             cols = gu_cols(i)
             for p in range(2):
-                even, odd = y[2 * p * RB:(2 * p + 1) * RB], y[(2 * p + 1) * RB:(2 * p + 2) * RB]
-                gk[p, :, cols] = jnp.where(core == 0, even, odd)
-                gd_s[layer, p, :, cols] = jnp.where(core == 0, odd, even).astype(BF16)
+                gk[p, :, cols] = y[p * RB:(p + 1) * RB]
+                gd_s[layer, p, :, cols] = y[(2 + p) * RB:(3 + p) * RB].astype(BF16)
             pltpu.make_async_remote_copy(gd_s.at[layer, :, :, cols], gd_r.at[layer, :, :, cols], gdsem.at[layer], gdrem.at[layer, i],
                                          device_id=dev(c, sibling), device_id_type=MESH).start()
 
@@ -523,8 +529,8 @@
                                          device_id=dev(c, sibling), device_id_type=MESH).wait_recv()
             s0 = gk[0, :, cols] + gd_r[layer, 0, :, cols].astype(F32)
             s1 = gk[1, :, cols] + gd_r[layer, 1, :, cols].astype(F32)
-            gk[0, :, cols] = jnp.where(chip == 0, s0, s1)
-            gx_s[layer, :, cols] = jnp.where(chip == 0, s1, s0).astype(BF16)
+            gk[0, :, cols] = s0
+            gx_s[layer, :, cols] = s1.astype(BF16)
             pltpu.make_async_remote_copy(gx_s.at[layer, :, cols], gx_r.at[layer, :, cols], gxsem.at[layer], gxrem.at[layer, i // (GT // NP)],
                                          device_id=dev(c, across), device_id_type=MESH).start()
 
@@ -533,12 +539,11 @@
             ref = gx_r.at[layer, :, pl.ds(q * width, width)]
             pltpu.make_async_remote_copy(ref, ref, gxsem.at[layer], gxrem.at[layer, q], device_id=dev(c, r), device_id_type=MESH).wait_recv()
             for j in range(2):
-                for w in range(2):
-                    lo = q * width + (2 * j + w) * 2 * CW
-                    mid, hi = lo + CW, lo + 2 * CW
-                    gate = (gk[0, :, lo:mid] + gx_r[layer, :, lo:mid].astype(F32)).astype(BF16).astype(F32)
-                    up = (gk[0, :, mid:hi] + gx_r[layer, :, mid:hi].astype(F32)).astype(BF16).astype(F32)
-                    aa_s[layer, q, j, :, w * CW:(w + 1) * CW] = (gate * jax.nn.sigmoid(gate) * up).astype(BF16)
+                lo = q * width + j * GB
+                mid, hi = lo + CW, lo + GB
+                gate = (gk[0, :, lo:mid] + gx_r[layer, :, lo:mid].astype(F32)).astype(BF16).astype(F32)
+                up = (gk[0, :, mid:hi] + gx_r[layer, :, mid:hi].astype(F32)).astype(BF16).astype(F32)
+                aa_s[layer, q, j] = (gate * jax.nn.sigmoid(gate) * up).astype(BF16)
             act_send(layer, q)
 
         ds_, dr_ = d_s.at[layer], d_r.at[layer]
@@ -555,18 +560,18 @@
                     if q < NP - 1:
                         dacc[:, lo:hi] = y
                         return
-                    for part in range(lo, hi, 2 * CW):
-                        rs_send(ds_, dr_, *dsem, part, y[:, part - lo:part - lo + 2 * CW])
+                    for part in range(lo, hi, CW):
+                        rs_send(ds_, dr_, *dsem, part, y[:, part - lo:part - lo + CW])
                 return run
 
             act_wait(layer, q)
             abuf[:, q * KD:(q + 1) * KD] = jnp.concatenate([aa_r[layer, q, p].astype(F32) for p in range(ROWS)], axis=0).astype(BF16)
-            for first, count in (((0, DN),) if q < NP - 1 else ((0, 4), (4, 2))):
+            for first, count in (((0, DN),) if q < NP - 1 else ((0, 1), (1, 1), (2, 1))):
                 run_phase(layer, BASE['d'] + q * DN + first, 0, 1, count, True, body(first))
 
-        run_phase(layer, BASE['gu'], 0, 6, 4, False, gu_body)
+        run_phase(layer, BASE['gu'], 0, 6, 2, False, gu_body)
         activate(0)
-        run_phase(layer, BASE['gu'], 6, GT, 4, False, gu_body)
+        run_phase(layer, BASE['gu'], 6, GT, 2, False, gu_body)
         activate(1)
         act_relay(layer, 0)
         for i in range(GT - LAG, GT):
@@ -611,6 +616,14 @@
                                          device_id=dev(c, r), device_id_type=MESH).wait_send()
 
 
+def finish_kernel(*refs):
+    copies = [pltpu.make_async_copy(refs[i], refs[4 + i], refs[8].at[i]) for i in range(4)]
+    for copy in copies:
+        copy.start()
+    for copy in copies:
+        copy.wait()
+
+
 def solution(mesh):
     hidden_spec = P('rep', 'row')
     index_spec = P(('rep', 'row'))
@@ -632,7 +645,7 @@
             V((LAYERS, D), BF16), V((LAYERS, D), BF16), V((ROWS * RB, D), BF16), V((ROWS * RB, FK), BF16), V((RB, QW), F32),
             V((QH * RB, HD), F32), V((KVH * RB, HD), F32), V((KVH * RB, HD), F32), V((QH * RB, HD), F32),
             V((2 * QH, CTX * KVH), jnp.int32), V((RB, HD), F32), V((RB, HD), F32),
-            V((ROWS, RB, 128), F32), V((3, ROWS, RB, 128), F32), V((ROWS, RB, D), BF16), V((2, RB, D), BF16),
+            V((RB, 128), F32), V((3, RB, 128), F32), V((ROWS, RB, D), BF16), V((2, RB, D), BF16),
             V((LAYERS, ROWS, RB, QKV_N), BF16), V((LAYERS, 3, RB, QKV_N), BF16),
             V((LAYERS, ROWS, RB, QW), BF16), V((LAYERS, 3, RB, QW), BF16),
             V((LAYERS, 2, RB, 2 * FF), BF16), V((LAYERS, 2, RB, 2 * FF), BF16), V((2, RB, 2 * FF), F32),
@@ -657,6 +670,13 @@
             compiler_params=pltpu.CompilerParams(collective_id=0, has_side_effects=True, vmem_limit_bytes=63000000),
         )(hidden_0, hidden_1, positions, lengths, cache_k.reshape(flat), cache_v.reshape(flat), norm_attn, norm_mlp,
           w_query, w_key, w_value, w_out, w_gate, w_up, w_down)
+        out = [pltpu.with_memory_space_constraint(o, pltpu.VMEM) for o in out]
+        out = pl.pallas_call(
+            finish_kernel,
+            out_shape=tuple(jax.ShapeDtypeStruct(shape, BF16) for shape in shapes),
+            in_specs=[vmem] * 4, out_specs=(any_spec,) * 4, scratch_shapes=[DMA((4,))],
+            compiler_params=pltpu.CompilerParams(vmem_limit_bytes=1 << 20),
+        )(*out)
         return out[0], out[1], out[2].reshape(cache_shape), out[3].reshape(cache_shape)
 
     return jax.shard_map(device_program, mesh=mesh,

time: 104 us -> 101 us (0.971)
  local copies, waits for them, and re-layouts: 3.18 us -> 0 us
    unnamed x4 -> x0, local copies, waits for them, and re-layouts: 3.18 us -> none
    pallas_call x0 -> x1, Pallas kernels: none -> 1.39 us  [device_program(): pl.pallas_call(finish_kernel, out_shape=tuple((jax.ShapeDtypeStruct(shape...]
    pallas_call x1, Pallas kernels: 100 us -> 99.2 us  [device_program(): pl.pallas_call(mega_kernel, out_shape=results, in_specs=[any_spec, any_sp...]
where the time goes in v4:
time: 101 us
  Pallas kernels  101 us (100%)
    pallas_call x1, Pallas kernels, device_program(): pl.pallas_call(mega_kernel, out_shape=results, in_specs=[any_spec, any_sp...  99.2 us

profile of v4, /device:TPU:0, one launch (start us, length us, event | category | flops | bytes accessed | tf_op | source)
XLA Modules:
  0.0 101.4 jit_solution(15155407126952350417)
XLA Ops:
  0.6 99.2 %shard_map.174 = (bf16[16,1536]{1,0:T(8,128)(2,1)S(1)}, bf16[16,1536]{1,0:T(8,128)(2,1)S(1)}, bf16[2,4,512,128]{3,2,1,0:T(8,128)(2,1)S(1)}, bf16[2,4,512,128]{3,2,1,0:T(8,128)(2,1)S(1)}) custom-call(bf16[16,1536]{1,0:T(8,128)(2,1)} %h0.1, bf16[16,1536]{1,0:T(8,128)(2,1)} %h1.1, s32[4]{0:T(128)} %positions.1, s32[4]{0:T(128)} %lengths.1, ...), custom_call_target="tpu_custom_call" | custom-call | tf_op jit(solution)/shard_map/pallas_call | solution.py:664
  99.8 1.4 %shard_map.175 = (bf16[16,1536]{1,0:T(8,128)(2,1)}, bf16[16,1536]{1,0:T(8,128)(2,1)}, bf16[2,4,512,128]{3,2,1,0:T(8,128)(2,1)}, bf16[2,4,512,128]{3,2,1,0:T(8,128)(2,1)}) custom-call(bf16[16,1536]{1,0:T(8,128)(2,1)S(1)} %get-tuple-element.12.refs_0_, bf16[16,1536]{1,0:T(8,128)(2,1)S(1)} %get-tuple-element.13.refs_1_, ...), custom_call_target="tpu_custom_call" | custom-call | tf_op jit(solution)/shard_map/pallas_call | solution.py:674

commit v5 on v4

--- a/solution.py
+++ b/solution.py
@@ -356,6 +356,8 @@
     lim_scr[...] = jnp.where(kv_of == srow_kv, slot - srow_step, 1 << 20)
 
     pltpu.make_async_remote_copy(is_recv, is_recv, isem.at[0], isem.at[1], device_id=dev(c, r), device_id_type=MESH).wait_recv()
+
+    own_lanes = jnp.right_shift(lane, 4) == rowi
 
     def normalise(p, xblock, total, gain):
         scale = lax.rsqrt(total * (1.0 / WIDTH) + EPS)[:, :1]
@@ -486,7 +488,7 @@
             last = layer == LAYERS - 1 and which == 1
             if not last:
                 sts, stv = st_s.at[layer, which], st_r.at[layer, which]
-                stat = jnp.broadcast_to(jnp.sum(squares, axis=1, keepdims=True), (RB, 128))
+                stat = jnp.sum(jnp.where(own_lanes, jnp.sum(squares, axis=1, keepdims=True), 0.0), axis=0, keepdims=True)
                 sts[...] = stat
                 stv[me] = stat
                 for e in range(1, COLS * ROWS):
@@ -500,7 +502,7 @@
             g = (gmbuf[layer:layer + 1, :] if which == 0 else gabuf[layer + 1:layer + 2, :]).astype(F32)
             parts = []
             for p in ((r, across, sibling, 2 * (1 - chip) + 1 - core) if which == 0 else range(ROWS)):
-                parts.append(normalise(p, xr[p].astype(F32), stv[p] + stv[ROWS + p], g))
+                parts.append(normalise(p, xr[p].astype(F32), jnp.max(jnp.where(own_lanes, stv[p] + stv[ROWS + p], 0.0), axis=1, keepdims=True), g))
             put_rows(nbuf, parts)
 
         run_phase(layer, BASE['o'], 0, 3, 1, False, o_body)
@@ -654,7 +656,7 @@
             V((LAYERS, 2, RB, D), BF16), V((LAYERS, ROWS, RB, D), BF16),
             V((LAYERS, 2, 2, RB, D), BF16), V((LAYERS, 2, ROWS, RB, D), BF16),
             V((LAYERS, NP, 2, RB, KD), BF16), V((LAYERS, NP, ROWS, RB, KD), BF16), V((LAYERS, NP, 2, RB, KD), BF16),
-            V((LAYERS, 2, RB, 128), F32), V((LAYERS, 2, COLS * ROWS, RB, 128), F32),
+            V((LAYERS, 2, 1, 128), F32), V((LAYERS, 2, COLS * ROWS, 1, 128), F32),
             DMA((NS,)), DMA((6,)), DMA((2,)), DMA((3,)),
             DMA((LAYERS, 3)), DMA((LAYERS, 4)), DMA((LAYERS, 3, 4)), DMA((LAYERS, 3, 4)), DMA((LAYERS, 2, 2)),
             DMA((LAYERS,)), DMA((LAYERS, GT)), DMA((LAYERS,)), DMA((LAYERS, NP)), DMA((LAYERS, NP, 7)), DMA((LAYERS, NP, 5)),

time: 101 us -> 101 us (level)
  Pallas kernels: 101 us -> 99.6 us
where the time goes in v5:
time: 101 us; the launch traced here: 100 us
  Pallas kernels  99.6 us (99%)
    pallas_call x1, Pallas kernels, device_program(): pl.pallas_call(mega_kernel, out_shape=results, in_specs=[any_spec, any_sp...  98.3 us

profile of v5, /device:TPU:0, one launch (start us, length us, event | category | flops | bytes accessed | tf_op | source)
XLA Modules:
  0.0 100.4 jit_solution(1806656917436275720)
XLA Ops:
  0.6 98.3 %shard_map.174 = (bf16[16,1536]{1,0:T(8,128)(2,1)S(1)}, bf16[16,1536]{1,0:T(8,128)(2,1)S(1)}, bf16[2,4,512,128]{3,2,1,0:T(8,128)(2,1)S(1)}, bf16[2,4,512,128]{3,2,1,0:T(8,128)(2,1)S(1)}) custom-call(bf16[16,1536]{1,0:T(8,128)(2,1)} %h0.1, bf16[16,1536]{1,0:T(8,128)(2,1)} %h1.1, s32[4]{0:T(128)} %positions.1, s32[4]{0:T(128)} %lengths.1, ...), custom_call_target="tpu_custom_call" | custom-call | tf_op jit(solution)/shard_map/pallas_call | solution.py:666
  98.9 1.4 %shard_map.175 = (bf16[16,1536]{1,0:T(8,128)(2,1)}, bf16[16,1536]{1,0:T(8,128)(2,1)}, bf16[2,4,512,128]{3,2,1,0:T(8,128)(2,1)}, bf16[2,4,512,128]{3,2,1,0:T(8,128)(2,1)}) custom-call(bf16[16,1536]{1,0:T(8,128)(2,1)S(1)} %get-tuple-element.12.refs_0_, bf16[16,1536]{1,0:T(8,128)(2,1)S(1)} %get-tuple-element.13.refs_1_, ...), custom_call_target="tpu_custom_call" | custom-call | tf_op jit(solution)/shard_map/pallas_call | solution.py:676
